TPU v7x, 32 devices: a 4x4x1 block of a 4x4x8 slice. The times are simulated.
32 devices in a mesh: data: 1 (over z), tp: 32 (over y, x, core).
Axes of the slice: x: 4, y: 4, z: 1, core: 2. Of those that a mesh axis runs over, the one named last changes fastest.
The devices are a block of a 4x4x8 slice.
Arguments:
- X: bfloat16 [2048, 2048], P(('data', 'tp'))
- gamma: float32 [2048], replicated
- W1: bfloat16 [2048, 32768], P(None, 'tp')
- W2: bfloat16 [32768, 2048], P('tp')
- dY: bfloat16 [2048, 2048], P(('data', 'tp'))
Outputs:
- output 1: bfloat16 [2048, 2048], P(('data', 'tp'))
- output 2: bfloat16 [2048, 2048], P(('data', 'tp'))
- output 3: float32 [2048, 32768], P('data', 'tp')
- output 4: float32 [32768, 2048], P(('data', 'tp'))
- output 5: float32 [2048], P('data')
All inputs are finite; a program needn't handle non-finite values.
Results may differ from a plain program's by a relative error of at most 0.00102.
Values are sent between devices in bfloat16 or wider.
A program may use at most 768 MiB of HBM per device.

v0:
```python
import jax
import jax.numpy as jnp
from jax import lax
from jax.sharding import PartitionSpec as P

EPS = 1e-6


def _gelu(a):
    return jax.nn.gelu(a, approximate=True)


def _ln(x):
    mu = jnp.mean(x, axis=-1, keepdims=True)
    xc = x - mu
    var = jnp.mean(xc * xc, axis=-1, keepdims=True)
    rstd = lax.rsqrt(var + EPS)
    return xc * rstd, rstd


def _tn(a, b):
    return lax.dot_general(a, b, (((0,), (0,)), ((), ())), preferred_element_type=jnp.float32)


def _nt(a, b):
    return lax.dot_general(a, b, (((1,), (1,)), ((), ())), preferred_element_type=jnp.float32)


def solution(mesh):
    rows = P(("data", "tp"), None)

    def body(X, gamma, W1, W2, dY):
        x = X.astype(jnp.float32)
        xhatv, rstd = _ln(x)
        Xn = lax.all_gather((xhatv * gamma).astype(jnp.bfloat16), "tp", axis=0, tiled=True)
        A = jnp.dot(Xn, W1, preferred_element_type=jnp.float32)
        H = _gelu(A).astype(jnp.bfloat16)
        Yp = jnp.dot(H, W2, preferred_element_type=jnp.float32)
        Y = (x + lax.psum_scatter(Yp, "tp", scatter_dimension=0, tiled=True)).astype(jnp.bfloat16)
        g = lax.all_gather(dY, "tp", axis=0, tiled=True)
        dW2 = _tn(H, g)
        dH = _nt(g, W2)
        dA = jax.vjp(_gelu, A)[1](dH)[0].astype(jnp.bfloat16)
        dW1 = _tn(Xn, dA)
        dXn = lax.psum_scatter(_nt(dA, W1), "tp", scatter_dimension=0, tiled=True)
        dgamma = lax.psum(jnp.sum(dXn * xhatv, axis=0), "tp")
        dxhat = dXn * gamma
        dx = rstd * (dxhat - jnp.mean(dxhat, axis=-1, keepdims=True) - xhatv * jnp.mean(dxhat * xhatv, axis=-1, keepdims=True))
        dX = (dY.astype(jnp.float32) + dx).astype(jnp.bfloat16)
        return Y, dX, dW1, dW2, dgamma

    return jax.shard_map(body, mesh=mesh,
                         in_specs=(rows, P(None), P(None, "tp"), P("tp", None), rows),
                         out_specs=(rows, rows, P("data", "tp"), rows, P("data")),
                         check_vma=False)
```

profile of v0, /device:TPU:97, one launch (start us, length us, event | category | flops | bytes accessed | tf_op | source)
XLA Modules:
  0.0 371.5 jit_solution(1647592784839529560)
XLA Ops:
  7.2 0.1 all-gather.5.cloned.1.call-start
  7.2 0.7 all-gather.5.cloned.1.call-update
  8.0 0.1 all-gather.3.cloned.1.call-start
  8.0 1.1 convert_reduce_fusion
  9.1 1.2 fusion.20
  10.4 1.8 fusion.13
  12.2 0.1 all-gather.3.cloned.1.call-update
  12.2 0.1 reduce-scatter.5.cloned.1.call-start
  12.3 49.4 %all-gather.5.cloned.1.call-done = bf16[2048,2048]{1,0:T(8,128)(2,1)} async-done(((bf16[64,2048]{1,0:T(8,128)(2,1)}), bf16[2048,2048]{1,0:T(8,128)(2,1)}) %all-gather.5.cloned.1.call-update) | async-done | bytes 8388624 | tf_op jit(solution)/shard_map/all_gather | solution.py:40
  61.7 14.6 %fusion.24 = f32[2048,1024]{1,0:T(8,128)} fusion(bf16[2048,2048]{1,0:T(8,128)(2,1)} %all-gather.5.cloned.1.call-done, bf16[1024,2048]{1,0:T(8,128)(2,1)} %param.8), kind=kOutput, calls=%fused_computation.35 | convolution fusion | flops 8589934592 | bytes 20971520 | tf_op jit(solution)/shard_map/dot_general | solution.py:26
  76.3 35.0 %all-gather.3.cloned.1.call-done = bf16[2048,2048]{1,0:T(8,128)(2,1)} async-done(((bf16[64,2048]{1,0:T(8,128)(2,1)}), bf16[2048,2048]{1,0:T(8,128)(2,1)}) %all-gather.3.cloned.1.call-update) | async-done | bytes 8388624 | tf_op jit(solution)/shard_map/all_gather | solution.py:35
  111.3 22.0 %fusion.6 = (bf16[2048,1024]{1,0:T(8,128)(2,1)S(1)}, f32[2048,1024]{1,0:T(8,128)}) fusion(f32[2048,1024]{1,0:T(8,128)} %fusion.24, bf16[2048,2048]{1,0:T(8,128)(2,1)} %all-gather.3.cloned.1.call-done, bf16[2048,1024]{1,0:T(8,128)(2,1)} %param.7), kind=kOutput, calls=%fused_computation.8 | convolution fusion | flops 8631877632 | bytes 33554432 | tf_op jit(solution)/shard_map/dot_general | solution.py:36
  133.2 2.0 copy-done.4
  135.3 11.7 %fusion.25 = f32[2048,2048]{1,0:T(8,128)} fusion(bf16[2048,1024]{1,0:T(8,128)(2,1)S(1)} %get-tuple-element.10, bf16[2048,1024]{1,0:T(8,128)(2,1)S(1)} %copy-done.3), kind=kOutput, calls=%fused_computation.36 | convolution fusion | flops 8589934592 | bytes 25165824 | tf_op jit(solution)/shard_map/dot_general | solution.py:26
  146.9 0.1 reduce-scatter.5.cloned.1.call-update
  147.0 0.2 reduce-scatter.3.cloned.1.call-start
  147.3 16.3 %fusion.23 = f32[2048,2048]{1,0:T(8,128)} fusion(bf16[1024,2048]{1,0:T(8,128)(2,1)} %param.8, f32[2048,1024]{1,0:T(8,128)} %get-tuple-element.11), kind=kOutput, calls=%fused_computation.34 | convolution fusion | flops 8608808960 | bytes 29360128 | tf_op jit(solution)/shard_map/dot_general | solution.py:38
  163.6 14.7 %fusion.26 = f32[2048,1024]{1,0:T(8,128)} fusion(bf16[2048,2048]{1,0:T(8,128)(2,1)} %all-gather.3.cloned.1.call-done, bf16[2048,1024]{1,0:T(8,128)(2,1)} %copy-done.4), kind=kOutput, calls=%fused_computation.37 | convolution fusion | flops 8589934592 | bytes 20971520 | tf_op jit(solution)/shard_map/dot_general | solution.py:22
  178.3 16.5 %fusion.22 = f32[1024,2048]{1,0:T(8,128)} fusion(bf16[2048,2048]{1,0:T(8,128)(2,1)} %all-gather.5.cloned.1.call-done, f32[2048,1024]{1,0:T(8,128)} %get-tuple-element.11), kind=kOutput, calls=%fused_computation.33 | convolution fusion | flops 8608808960 | bytes 25165824 | tf_op jit(solution)/shard_map/dot_general | solution.py:22
  194.7 57.4 %reduce-scatter.5.cloned.1.call-done = f32[64,2048]{1,0:T(8,128)} async-done(((f32[2048,2048]{1,0:T(8,128)}), f32[64,2048]{1,0:T(8,128)}) %reduce-scatter.5.cloned.1.call-update) | async-done | bytes 524304 | tf_op jit(solution)/shard_map/reduce_scatter | solution.py:45
  252.2 1.4 fusion.19
  253.6 46.3 %psum.7 = f32[2048]{0:T(1024)} all-reduce(f32[2048]{0:T(1024)S(1)} %get-tuple-element.5), channel_id=1, replica_groups=mesh['data'=1,'tp'=32] {'tp'}, use_global_device_ids=true, to_apply=%region_7.0 | all-reduce | flops 2048 | bytes 16384 | tf_op jit(solution)/shard_map/psum | solution.py:46
  299.9 62.8 %reduce-scatter.3.cloned.1.call-done = f32[64,2048]{1,0:T(8,128)} async-done(((f32[2048,2048]{1,0:T(8,128)}), f32[64,2048]{1,0:T(8,128)}) %reduce-scatter.3.cloned.1.call-update) | async-done | bytes 524304 | tf_op jit(solution)/shard_map/reduce_scatter | solution.py:39
  362.7 2.3 fusion.18
  (13 shorter events, 0.1 us)
Async XLA Ops:
  7.2 54.6 %all-gather.5.cloned.1.call-start = ((), (), s32[]{:S(2)}) async-start(), calls=%async_computation.4 | async-start | bytes 8650752 | tf_op jit(solution)/shard_map/all_gather | solution.py:40
  8.0 103.3 %all-gather.3.cloned.1.call-start = ((), (), s32[]{:S(2)}) async-start(), calls=%async_computation.2 | async-start | bytes 8650752 | tf_op jit(solution)/shard_map/all_gather | solution.py:35
  12.2 240.0 %reduce-scatter.5.cloned.1.call-start = ((), (), s32[]{:S(2)}) async-start(), calls=%async_computation.5 | async-start | bytes 17301504 | tf_op jit(solution)/shard_map/reduce_scatter | solution.py:45
  111.3 24.0 %copy-start.3 = (bf16[2048,1024]{1,0:T(8,128)(2,1)S(1)}, bf16[2048,1024]{1,0:T(8,128)(2,1)}, u32[]{:S(2)}) copy-start(bf16[2048,1024]{1,0:T(8,128)(2,1)} %param.7) | copy-start | bytes 12582916
  133.2 2.0 copy-start.4
  147.0 215.6 %reduce-scatter.3.cloned.1.call-start = ((), (), s32[]{:S(2)}) async-start(), calls=%async_computation.3 | async-start | bytes 17301504 | tf_op jit(solution)/shard_map/reduce_scatter | solution.py:39
  178.3 73.9 %copy-start = (bf16[64,2048]{1,0:T(8,128)(2,1)S(1)}, bf16[64,2048]{1,0:T(8,128)(2,1)}, u32[]{:S(2)}) copy-start(bf16[64,2048]{1,0:T(8,128)(2,1)} %param.5) | copy-start | bytes 786436
  178.3 73.9 %copy-start.2 = (f32[2048]{0:T(1024)S(1)}, f32[2048]{0:T(1024)}, u32[]{:S(2)}) copy-start(f32[2048]{0:T(1024)} %param.6) | copy-start | bytes 24580
  178.3 184.4 %copy-start.1 = (bf16[64,2048]{1,0:T(8,128)(2,1)S(1)}, bf16[64,2048]{1,0:T(8,128)(2,1)}, u32[]{:S(2)}) copy-start(bf16[64,2048]{1,0:T(8,128)(2,1)} %param.9) | copy-start | bytes 786436
Sparse Core Ops, SparseCore 0:
  10.1 51.5 all-gather.4
  64.4 46.8 all-gather.2
  147.1 105.0 reduce-scatter.4
  255.8 106.8 reduce-scatter.2
where the time goes:
time: 372 us
  waiting for transfers between devices  206 us (55%)
  matrix products  95.6 us (26%)
  blocking collectives  46.3 us (12%)
  between operations  13.8 us (4%)
  other arithmetic  7.85 us (2%)
    reduce_scatter x1, waiting for transfers between devices, body(): lax.psum_scatter(Yp, 'tp', scatter_dimension=0, tiled=True)  62.8 us
    reduce_scatter x1, waiting for transfers between devices, body(): dXn = lax.psum_scatter(_nt(dA, W1), 'tp', scatter_dimension=0, tiled=True)  57.4 us
    all_gather x1, waiting for transfers between devices, body(): g = lax.all_gather(dY, 'tp', axis=0, tiled=True)  49.4 us
    psum x1, blocking collectives, body(): dgamma = lax.psum(jnp.sum(dXn * xhatv, axis=0), 'tp')  46.3 us
    all_gather x1, waiting for transfers between devices, body(): lax.all_gather((xhatv * gamma).astype(jnp.bfloat16), 'tp', axis=0, tiled=...  35 us
    dot_general x2, matrix products, _tn(): lax.dot_general(a, b, (((0,), (0,)), ((), ())), preferred_element_type=jn...  31.1 us
    dot_general x2, matrix products, _nt(): lax.dot_general(a, b, (((1,), (1,)), ((), ())), preferred_element_type=jn...  26.2 us
    dot_general x1, matrix products, body(): A = jnp.dot(Xn, W1, preferred_element_type=jnp.float32)  22 us
  transfers between devices with their start and end apart: 4, of which 4 were waited for; matrix products, arithmetic and copies ran while one was open for 18% of the time, Pallas kernels for 0%

commit v1 on v0

v1 whole, which is shorter than its diff:
```python
import math

import jax
import jax.numpy as jnp
from jax import lax
from jax.experimental import pallas as pl
from jax.experimental.pallas import tpu as pltpu
from jax.sharding import PartitionSpec as P

EPS = 1e-6
BF16 = jnp.bfloat16
F32 = jnp.float32
MESH = pl.DeviceIdType.MESH

REL = (0, 1, -1, 2)
IX = {0: 0, 1: 1, -1: 2, 2: 3}
ORDER = (0, 1, -1, 2)
SIDE = 4


def _dot(a, b, ca, cb):
    return lax.dot_general(a, b, (((ca,), (cb,)), ((), ())), preferred_element_type=F32)


def _ln(x):
    mu = jnp.mean(x, axis=-1, keepdims=True)
    xc = x - mu
    var = jnp.mean(xc * xc, axis=-1, keepdims=True)
    rstd = lax.rsqrt(var + EPS)
    return xc * rstd, rstd


def _gelu_and_grad(a):
    c = math.sqrt(2.0 / math.pi)
    a2 = a * a
    t = jnp.tanh(c * (a + 0.044715 * (a2 * a)))
    cdf = 0.5 * (1.0 + t)
    grad = cdf + (0.5 * a * (1.0 - t * t)) * (c + (3.0 * 0.044715 * c) * a2)
    return a * cdf, grad


def _kernel(x_ref, g_ref, w1_hbm, w2_hbm, dy_hbm,
            y_out, dx_out, dg_out, dw1_hbm, dw2_hbm,
            xn, dy, h, da, w1, w2, acc, zbuf, stage, sibr, r1, r2, ysum, gam, gin, dwst,
            ags, agr, p1s, p1r, p2s, p2r, sbs, sbr, gs, gr, lsem, c1, c2, csib):
    me = lax.axis_index("tp")
    core = me % 2
    cx = (me // 2) % SIDE
    cy = me // (2 * SIDE)

    def dev(yy, xx, cc):
        return {"tp": ((yy % SIDE) * SIDE + (xx % SIDE)) * 2 + cc}

    yp, ym, yf = dev(cy + 1, cx, core), dev(cy + SIDE - 1, cx, core), dev(cy + 2, cx, core)
    xp, xm, xf = dev(cy, cx + 1, core), dev(cy, cx + SIDE - 1, core), dev(cy, cx + 2, core)
    sib = dev(cy, cx, 1 - core)

    R = x_ref.shape[0]
    HR = R // 2
    D = x_ref.shape[1]
    FS = w1.shape[1]
    BLK = 2 * SIDE * R
    OWN = SIDE * R
    C = D // 2
    Q = C // 4

    cw1 = pltpu.make_async_copy(w1_hbm, w1, lsem.at[0])
    cw2 = pltpu.make_async_copy(w2_hbm, w2, lsem.at[1])
    cdy = pltpu.make_async_copy(dy_hbm, dy.at[pl.ds(0, R)], lsem.at[2])
    cdy.start()
    cw1.start()
    cw2.start()
    xhat, rstd = _ln(x_ref[...].astype(F32))
    xn[0:R, :] = (xhat * g_ref[...]).astype(BF16)

    bar = pltpu.get_barrier_semaphore()
    for d in (yp, ym, yf, xp, xm, xf, sib):
        pl.semaphore_signal(bar, inc=1, device_id=d, device_id_type=MESH)
    pl.semaphore_wait(bar, 7)

    def remote(src, dst, ss, rs, d):
        return pltpu.make_async_remote_copy(src_ref=src, dst_ref=dst, send_sem=ss, recv_sem=rs, device_id=d, device_id_type=MESH)

    pending = []

    def go(c):
        c.start()
        pending.append(c)

    class Gather:
        def __init__(self, buf, first, second, xfirst, base):
            n = [base]

            def at(r1_, r2_, half=None):
                dd, ee = (r2_, r1_) if xfirst else (r1_, r2_)
                o = (IX[dd] * 2 * SIDE + IX[ee]) * R
                if half is None:
                    return buf.at[pl.ds(o, R)]
                return buf.at[pl.ds(o + half * HR, HR)]

            def mk(src, dst, d):
                i = n[0]
                n[0] += 1
                return remote(src, dst, ags.at[i], agr.at[i], d)

            (fp, fm), (sp, sm) = first, second
            self.d1p = mk(at(0, 0), at(-1, 0), fp)
            self.d1m = mk(at(0, 0), at(1, 0), fm)
            self.d1hp = mk(at(-1, 0, 0), at(2, 0, 0), fp)
            self.d1hm = mk(at(1, 0, 1), at(2, 0, 1), fm)
            self.d2p = {r: mk(at(r, 0), at(r, -1), sp) for r in REL}
            self.d2m = {r: mk(at(r, 0), at(r, 1), sm) for r in REL}
            self.d2hp = {r: mk(at(r, -1, 0), at(r, 2, 0), sp) for r in REL}
            self.d2hm = {r: mk(at(r, 1, 1), at(r, 2, 1), sm) for r in REL}
            self.sb = {r: mk(buf.at[pl.ds(IX[r] * BLK, OWN)], buf.at[pl.ds(IX[r] * BLK + OWN, OWN)], sib) for r in REL}

    gx = Gather(xn, (xp, xm), (yp, ym), True, 0)
    gy = Gather(dy, (yp, ym), (xp, xm), False, 24)

    cdy.wait()
    for g in (gx, gy):
        go(g.d1p)
        go(g.d1m)
    for g in (gx, gy):
        go(g.d2p[0])
        go(g.d2m[0])
    for g in (gx, gy):
        g.d1p.wait_recv()
        go(g.d1hp)
        g.d1m.wait_recv()
        go(g.d1hm)
    for r in (1, -1):
        for g in (gx, gy):
            go(g.d2p[r])
            go(g.d2m[r])
    gy.d2p[0].wait_recv()
    go(gy.d2hp[0])
    gy.d2m[0].wait_recv()
    go(gy.d2hm[0])
    for g in (gx, gy):
        g.d1hp.wait_recv()
        g.d1hm.wait_recv()
        go(g.d2p[2])
        go(g.d2m[2])
    go(gx.sb[0])
    gy.d2hp[0].wait_recv()
    gy.d2hm[0].wait_recv()
    go(gy.sb[0])

    TF = 512

    def hidden(dd):
        o = IX[dd] * BLK

        def step(f, _):
            fo = pl.multiple_of(f * TF, TF)
            a = _dot(xn[o:o + BLK, :], w1[:, pl.ds(fo, TF)], 1, 0)
            dh = _dot(dy[o:o + BLK, :], w2[pl.ds(fo, TF), :], 1, 1)
            hv, gv = _gelu_and_grad(a)
            h[o:o + BLK, pl.ds(fo, TF)] = hv.astype(BF16)
            da[o:o + BLK, pl.ds(fo, TF)] = (gv * dh).astype(BF16)
            return 0

        lax.fori_loop(0, FS // TF, step, 0)

    cw1.wait()
    cw2.wait()
    gx.sb[0].wait_recv()
    gy.sb[0].wait_recv()
    hidden(0)

    for e in (0, -1, 1):
        gx.d2p[e].wait_recv()
        go(gx.d2hp[e])
        gx.d2m[e].wait_recv()
        go(gx.d2hm[e])
    for r in (1, -1):
        gy.d2p[r].wait_recv()
        go(gy.d2hp[r])
        gy.d2m[r].wait_recv()
        go(gy.d2hm[r])
    gx.d2p[2].wait_recv()
    go(gx.d2hp[2])
    gx.d2m[2].wait_recv()
    go(gx.d2hm[2])
    go(gx.sb[1])
    go(gx.sb[-1])
    gy.d2hp[1].wait_recv()
    gy.d2hm[1].wait_recv()
    go(gy.sb[1])
    gy.d2p[2].wait_recv()
    go(gy.d2hp[2])
    gy.d2m[2].wait_recv()
    go(gy.d2hm[2])
    gx.sb[1].wait_recv()
    gy.sb[1].wait_recv()
    hidden(1)
    gy.d2hp[-1].wait_recv()
    gy.d2hm[-1].wait_recv()
    go(gy.sb[-1])
    gx.sb[-1].wait_recv()
    gy.sb[-1].wait_recv()
    hidden(-1)
    for e in REL:
        gx.d2hp[e].wait_recv()
        gx.d2hm[e].wait_recv()
    go(gx.sb[2])
    gy.d2hp[2].wait_recv()
    gy.d2hm[2].wait_recv()
    go(gy.sb[2])
    gx.sb[2].wait_recv()
    gy.sb[2].wait_recv()
    hidden(2)

    live = {}

    def partial_block(k, i):
        s, slot, col, o = k % 2, i % 2, (k % 2) * C, i * BLK

        def step(n, _):
            if k < 2:
                co = pl.multiple_of(col + n * (2 * Q), 2 * Q)
                t = _dot(h[o:o + BLK, :], w2[:, pl.ds(co, 2 * Q)], 1, 0)
            else:
                co = pl.multiple_of(col + n * (2 * Q), 2 * Q)
                t = _dot(da[o:o + BLK, :], w1[pl.ds(co, 2 * Q), :], 1, 1)
            for j in range(2):
                acc[s, 2 * n + j, i] = t[:OWN, j * Q:(j + 1) * Q].reshape(SIDE, R, Q)
                stage[slot, 2 * n + j] = t[OWN:, j * Q:(j + 1) * Q].reshape(SIDE, R, Q)
            return 0

        lax.fori_loop(0, 2, step, 0)

    def partials(k):
        s = k % 2
        if k >= 2:
            for c in live.pop(("p1", k - 2)):
                c.wait_send()
        cs = [remote(stage.at[i % 2], sibr.at[i], sbs.at[i], sbr.at[i], sib) for i in range(SIDE)]

        def add(i):
            cs[i].wait_recv()
            for q in range(4):
                acc[s, q, i] = acc[s, q, i] + sibr[i, q]
            if k < 3:
                pl.semaphore_signal(csib, inc=1, device_id=sib, device_id_type=MESH)

        for i in range(SIDE):
            if i >= 2:
                cs[i - 2].wait_send()
            partial_block(k, i)
            if k > 0:
                pl.semaphore_wait(csib, 1)
            cs[i].start()
            if i >= 1:
                add(i - 1)
        add(SIDE - 1)
        cs[2].wait_send()
        cs[3].wait_send()

    YR, XR = (yp, ym), (xp, xm)

    def ring_copies(get, buf, ss, rs, ring):
        plus, minus = ring
        src = [(get(0, 2), plus), (get(1, 2), minus), (get(1, 1), plus), (get(0, -1), minus), (get(0, 1), plus), (get(1, -1), minus)]
        return [remote(v, buf.at[j], ss.at[j], rs.at[j], d) for j, (v, d) in enumerate(src)]

    def p1_get(k, ab):
        if ab == 0:
            return lambda p, r: acc.at[k % 2, p, IX[r]]
        return lambda p, r: acc.at[k % 2, 2 + p, :, IX[r]]

    def p2_get(k, ab):
        return lambda p, r: zbuf.at[k % 2, 2 * ab + p, IX[r]]

    def e1(k):
        if k >= 2:
            pl.semaphore_wait(c1.at[0], 1)
            pl.semaphore_wait(c1.at[1], 1)
            pl.semaphore_wait(c1.at[2], 1)
            pl.semaphore_wait(c1.at[3], 1)
        s = k % 2
        cs = [ring_copies(p1_get(k, ab), r1.at[s, ab], p1s.at[s, ab], p1r.at[s, ab], (YR, XR)[ab]) for ab in range(2)]
        live["c1", k] = cs
        for j in range(4):
            for ab in range(2):
                cs[ab][j].start()

    def forward(get, buf, cs, ab):
        cs[ab][0].wait_recv()
        v = get(0, 1)
        v[...] = v[...] + buf[ab, 0]
        cs[ab][4].start()
        cs[ab][1].wait_recv()
        v = get(1, -1)
        v[...] = v[...] + buf[ab, 1]
        cs[ab][5].start()

    def final(get, buf, cs, ab):
        for j in (2, 3, 4, 5):
            cs[ab][j].wait_recv()
        return (get(0, 0)[...] + buf[ab, 3] + buf[ab, 4], get(1, 0)[...] + buf[ab, 2] + buf[ab, 5])

    def credit(c):
        for i, d in enumerate((ym, yp, xm, xp)):
            pl.semaphore_signal(c.at[i], inc=1, device_id=d, device_id_type=MESH)

    def e2(k):
        cs = live["c1", k]
        for ab in range(2):
            forward(p1_get(k, ab), r1.at[k % 2], cs, ab)

    def e3(k):
        s = k % 2
        cs = live["c1", k]
        if k >= 2:
            for c in live.pop(("p2", k - 2)):
                c.wait_send()
            for i in range(4):
                pl.semaphore_wait(c2.at[i], 1)
        ds = [ring_copies(p2_get(k, ab), r2.at[s, ab], p2s.at[s, ab], p2r.at[s, ab], (XR, YR)[ab]) for ab in range(2)]
        live["c2", k] = ds
        for ab in range(2):
            a, b = final(p1_get(k, ab), r1.at[s], cs, ab)
            zbuf[s, 2 * ab] = a
            zbuf[s, 2 * ab + 1] = b
            for j in range(4):
                ds[ab][j].start()
        live["p1", k] = [c for v in cs for c in v]
        if k < 2:
            credit(c1)

    def e4(k):
        cs = live["c2", k]
        for ab in range(2):
            forward(p2_get(k, ab), r2.at[k % 2], cs, ab)

    def e5(k):
        cs = live["c2", k]
        for ab in range(2):
            a, b = final(p2_get(k, ab), r2.at[k % 2], cs, ab)
            o = (k % 2) * C + 2 * ab * Q
            ysum[:, o:o + Q] = a
            ysum[:, o + Q:o + 2 * Q] = b
        live["p2", k] = [c for v in cs for c in v]
        if k < 2:
            credit(c2)

    TM = dwst.shape[1]

    def dw2_copy(i):
        r = pl.multiple_of((i // 2) * TM, TM)
        c = pl.multiple_of((i % 2) * FS, FS)
        return pltpu.make_async_copy(dwst.at[i % 2], dw2_hbm.at[pl.ds(r, TM), pl.ds(c, FS)], lsem.at[3 + i % 2])

    def dw1_copy(i):
        r = pl.multiple_of(i * TM, TM)
        return pltpu.make_async_copy(dwst.at[i % 2], dw1_hbm.at[pl.ds(r, TM), :], lsem.at[3 + i % 2])

    def dw2_tile(i):
        r = pl.multiple_of((i // 2) * TM, TM)
        c = pl.multiple_of((i % 2) * FS, FS)
        return _dot(h[:, pl.ds(r, TM)], dy[:, pl.ds(c, FS)], 0, 0)

    def dw1_tile(i):
        r = pl.multiple_of(i * TM, TM)
        return _dot(xn[:, pl.ds(r, TM)], da[...], 0, 0)

    def dw(copy, tile, lo, hi, first):
        def step(i, _):
            @pl.when(i >= first)
            def _():
                copy(i - 2).wait()
            dwst[i % 2] = tile(i)
            copy(i).start()
            return 0

        lax.fori_loop(lo, hi, step, 0)

    NT2 = FS // TM * (D // FS)
    NT1 = D // TM

    partials(0)
    e1(0)
    partials(1)
    e2(0)
    e1(1)
    dw(dw2_copy, dw2_tile, 0, NT2 // 2, 2)
    e3(0)
    partials(2)
    e2(1)
    e1(2)
    e4(0)
    dw(dw2_copy, dw2_tile, NT2 // 2, NT2, 2)
    dw2_copy(NT2 - 2).wait()
    dw2_copy(NT2 - 1).wait()
    e5(0)
    e3(1)
    partials(3)
    e2(2)
    e1(3)
    e4(1)
    dw(dw1_copy, dw1_tile, 0, NT1 // 2, 2)
    e5(1)
    y_out[...] = (x_ref[...].astype(F32) + ysum[...]).astype(BF16)
    e3(2)
    dw(dw1_copy, dw1_tile, NT1 // 2, NT1, 2)
    e2(3)
    e4(2)
    dw1_copy(NT1 - 2).wait()
    dw1_copy(NT1 - 1).wait()
    e5(2)
    e3(3)
    e4(3)
    e5(3)

    xhat, rstd = _ln(x_ref[...].astype(F32))
    dxn = ysum[...]
    gam[0] = jnp.sum(dxn * xhat, axis=0, keepdims=True)
    cs = [remote(gam.at[0], gin.at[0], gs.at[0], gr.at[0], sib)]
    cs += [remote(gam.at[1], gin.at[1 + j], gs.at[1 + j], gr.at[1 + j], d) for j, d in enumerate((xp, xm, xf))]
    cs += [remote(gam.at[2], gin.at[4 + j], gs.at[4 + j], gr.at[4 + j], d) for j, d in enumerate((yp, ym, yf))]
    cs[0].start()
    dxhat = dxn * g_ref[...]
    dx = rstd * (dxhat - jnp.mean(dxhat, axis=-1, keepdims=True) - xhat * jnp.mean(dxhat * xhat, axis=-1, keepdims=True))
    dx_out[...] = (dy[0:R, :].astype(F32) + dx).astype(BF16)
    cs[0].wait_recv()
    gam[1] = gam[0] + gin[0]
    for j in (1, 2, 3):
        cs[j].start()
    for j in (1, 2, 3):
        cs[j].wait_recv()
    gam[2] = gam[1] + gin[1] + gin[2] + gin[3]
    for j in (4, 5, 6):
        cs[j].start()
    for j in (4, 5, 6):
        cs[j].wait_recv()
    dg_out[...] = gam[2] + gin[4] + gin[5] + gin[6]
    for c in cs + pending:
        c.wait_send()
    for key in (("p1", 2), ("p1", 3), ("p2", 2), ("p2", 3)):
        for c in live.pop(key):
            c.wait_send()


def solution(mesh):
    rows = P(("data", "tp"), None)
    assert mesh.shape["tp"] == 2 * SIDE * SIDE

    def body(X, gamma, W1, W2, dY):
        R, D = X.shape
        FS = W1.shape[1]
        T = R * 2 * SIDE * SIDE
        C = D // 2
        Q = C // 4
        vm = pl.BlockSpec(memory_space=pltpu.VMEM)
        anyspace = pl.BlockSpec(memory_space=pl.ANY)
        dma = pltpu.SemaphoreType.DMA
        reg = pltpu.SemaphoreType.REGULAR
        Y, dX, dg, dW1, dW2 = pl.pallas_call(
            _kernel,
            out_shape=(
                jax.ShapeDtypeStruct((R, D), BF16),
                jax.ShapeDtypeStruct((R, D), BF16),
                jax.ShapeDtypeStruct((1, D), F32),
                jax.ShapeDtypeStruct((D, FS), F32),
                jax.ShapeDtypeStruct((FS, D), F32),
            ),
            in_specs=[vm, vm, anyspace, anyspace, anyspace],
            out_specs=(vm, vm, vm, anyspace, anyspace),
            scratch_shapes=[
                pltpu.VMEM((T, D), BF16),
                pltpu.VMEM((T, D), BF16),
                pltpu.VMEM((T, FS), BF16),
                pltpu.VMEM((T, FS), BF16),
                pltpu.VMEM((D, FS), BF16),
                pltpu.VMEM((FS, D), BF16),
                pltpu.VMEM((2, 4, SIDE, SIDE, R, Q), F32),
                pltpu.VMEM((2, 4, SIDE, R, Q), F32),
                pltpu.VMEM((2, 4, SIDE, R, Q), F32),
                pltpu.VMEM((SIDE, 4, SIDE, R, Q), F32),
                pltpu.VMEM((2, 2, 6, SIDE, R, Q), F32),
                pltpu.VMEM((2, 2, 6, R, Q), F32),
                pltpu.VMEM((R, D), F32),
                pltpu.VMEM((3, 1, D), F32),
                pltpu.VMEM((7, 1, D), F32),
                pltpu.VMEM((2, 256, FS), F32),
                dma((48,)), dma((48,)),
                dma((2, 2, 6)), dma((2, 2, 6)),
                dma((2, 2, 6)), dma((2, 2, 6)),
                dma((SIDE,)), dma((SIDE,)),
                dma((7,)), dma((7,)),
                dma((5,)),
                reg((4,)), reg((4,)), reg,
            ],
            compiler_params=pltpu.CompilerParams(
                collective_id=0, has_side_effects=True, vmem_limit_bytes=67043328),
        )(X, gamma.reshape(1, D), W1, W2, dY)
        return Y, dX, dW1, dW2, dg.reshape(D)

    return jax.shard_map(body, mesh=mesh,
                         in_specs=(rows, P(None), P(None, "tp"), P("tp", None), rows),
                         out_specs=(rows, rows, P("data", "tp"), rows, P("data")),
                         check_vma=False)
```

time: 372 us -> 218 us (0.59)
  waiting for transfers between devices: 206 us -> 0 us
  Pallas kernels: 0 us -> 201 us
  matrix products: 95.6 us -> 0 us
  blocking collectives: 46.3 us -> 0 us
  local copies, waits for them, and re-layouts: 2.03 us -> 16.1 us
  between operations: 13.8 us -> 0.65 us
  other arithmetic: 7.85 us -> 0.01 us
    pallas_call x0 -> x1, Pallas kernels: none -> 201 us  [body(): pl.pallas_call(_kernel, out_shape=(jax.ShapeDtypeStruct((R, D), BF16), ja...]
    reduce_scatter x2 -> x0, waiting for transfers between devices: 120 us -> none  [the longest x1 62.8 us: body(): lax.psum_scatter(Yp, 'tp', scatter_dimension=0, tiled=True)]
    dot_general x6 -> x0, matrix products: 95.6 us -> none  [the longest x2 31.1 us: _tn(): lax.dot_general(a, b, (((0,), (0,)), ((), ())), preferred_element_type=jn...]
    all_gather x2 -> x0, waiting for transfers between devices: 84.4 us -> none  [the longest x1 49.4 us: body(): g = lax.all_gather(dY, 'tp', axis=0, tiled=True)]
    psum x1 -> x0, blocking collectives: 46.3 us -> none  [body(): dgamma = lax.psum(jnp.sum(dXn * xhatv, axis=0), 'tp')]
    unnamed x10 -> x11, local copies, waits for them, and re-layouts: 2.03 us -> 16.1 us
    convert_element_type x2 -> x0, other arithmetic: 4.15 us -> none  [the longest x1 2.34 us: body(): dX = (dY.astype(jnp.float32) + dx).astype(jnp.bfloat16)]
  transfers between devices with their start and end apart: 4 -> 0, of which waited for: 4 -> 0; matrix products, arithmetic and copies ran while one was open for 18% -> 0% of each run, Pallas kernels for 0% -> 0%
where the time goes in v1:
time: 218 us
  Pallas kernels  201 us (92%)
  local copies, waits for them, and re-layouts  16.1 us (7%)
    pallas_call x1, Pallas kernels, body(): pl.pallas_call(_kernel, out_shape=(jax.ShapeDtypeStruct((R, D), BF16), ja...  201 us
    unnamed x11, local copies, waits for them, and re-layouts  16.1 us

profile of v1, /device:TPU:97, one launch (start us, length us, event | category | flops | bytes accessed | tf_op | source)
XLA Modules:
  0.0 218.1 jit_solution(11934799740541898342)
XLA Ops:
  0.6 201.3 %shard_map.92 = (bf16[64,2048]{1,0:T(8,128)(2,1)}, bf16[64,2048]{1,0:T(8,128)(2,1)}, f32[1,2048]{1,0:T(1,128)}, f32[2048,1024]{1,0:T(8,128)}, f32[1024,2048]{1,0:T(8,128)}) custom-call(bf16[64,2048]{1,0:T(8,128)(2,1)} %x_ref.1, f32[1,2048]{1,0:T(1,128)} %bitcast.4, bf16[2048,1024]{1,0:T(8,128)(2,1)} %w1_hbm.1, bf16[1024,2048]{1,0:T(8,128)(2,1)} %w2_hbm.1, ...), custom_call_target="tpu_custom_call" | custom-call | tf_op jit(solution)/shard_map/pallas_call | solution.py:460
  202.0 1.7 copy.15
  203.6 0.0 slice-start
  203.6 1.8 copy.16
  205.5 0.0 slice-start.1
  205.5 8.6 %copy.17 = f32[2048,1024]{1,0:T(8,128)} copy(f32[2048,1024]{1,0:T(8,128)} %get-tuple-element.22) | data formatting | bytes 16777216
  214.1 0.0 slice-done
  214.1 0.0 slice-done.1
  214.1 0.0 copy-start
  214.1 3.4 %copy.18 = f32[1024,2048]{1,0:T(8,128)} copy(f32[1024,2048]{1,0:T(8,128)S(1)} %bitcast.3) | data formatting | bytes 16777216
  217.5 0.0 copy-done
  217.5 0.6 copy.19
  (1 shorter events, 0.0 us)
Async XLA Ops:
  203.6 10.4 %slice-start = ((s8[8388608]{0:T(1024)(128)(4,1)}), s8[4194304]{0:T(1024)(128)(4,1)S(1)}, s32[]{:S(2)}) async-start(s8[8388608]{0:T(1024)(128)(4,1)} %bitcast.2), calls=%async_computation | async-start | bytes 8388608
  205.5 8.6 %slice-start.1 = ((s8[8388608]{0:T(1024)(128)(4,1)}), s8[4194304]{0:T(1024)(128)(4,1)S(1)}, s32[]{:S(2)}) async-start(s8[8388608]{0:T(1024)(128)(4,1)} %bitcast.2), calls=%async_computation.1 | async-start | bytes 8388608
  214.1 3.4 %copy-start = (f32[1,2048]{1,0:T(1,128)S(1)}, f32[1,2048]{1,0:T(1,128)}, u32[]{:S(2)}) copy-start(f32[1,2048]{1,0:T(1,128)} %get-tuple-element.14) | copy-start | bytes 24580

commit v2 on v1

v2 whole, which is shorter than its diff:
```python
import math

import jax
import jax.numpy as jnp
from jax import lax
from jax.experimental import pallas as pl
from jax.experimental.pallas import tpu as pltpu
from jax.sharding import PartitionSpec as P

EPS = 1e-6
BF16 = jnp.bfloat16
F32 = jnp.float32
MESH = pl.DeviceIdType.MESH

REL = (0, 1, -1, 2)
IX = {0: 0, 1: 1, -1: 2, 2: 3}
ORDER = (0, 1, -1, 2)
SIDE = 4


def _dot(a, b, ca, cb):
    return lax.dot_general(a, b, (((ca,), (cb,)), ((), ())), preferred_element_type=F32)


def _ln(x):
    mu = jnp.mean(x, axis=-1, keepdims=True)
    xc = x - mu
    var = jnp.mean(xc * xc, axis=-1, keepdims=True)
    rstd = lax.rsqrt(var + EPS)
    return xc * rstd, rstd


def _gelu_and_grad(a):
    c = math.sqrt(2.0 / math.pi)
    a2 = a * a
    t = jnp.tanh(c * (a + 0.044715 * (a2 * a)))
    cdf = 0.5 * (1.0 + t)
    grad = cdf + (0.5 * a * (1.0 - t * t)) * (c + (3.0 * 0.044715 * c) * a2)
    return a * cdf, grad


def _kernel(x_ref, g_ref, w1_hbm, w2_hbm, dy_hbm,
            y_out, dx_out, dg_out, dw1_hbm, dw2_hbm,
            xn, dy, h, da, w1, w2, acc, zbuf, stage, sibr, r1, r2, ysum, gam, gin, dwst,
            ags, agr, p1s, p1r, p2s, p2r, sbs, sbr, gs, gr, lsem, c1, c2, csib):
    me = lax.axis_index("tp")
    core = me % 2
    cx = (me // 2) % SIDE
    cy = me // (2 * SIDE)

    def dev(yy, xx, cc):
        return {"tp": ((yy % SIDE) * SIDE + (xx % SIDE)) * 2 + cc}

    yp, ym, yf = dev(cy + 1, cx, core), dev(cy + SIDE - 1, cx, core), dev(cy + 2, cx, core)
    xp, xm, xf = dev(cy, cx + 1, core), dev(cy, cx + SIDE - 1, core), dev(cy, cx + 2, core)
    sib = dev(cy, cx, 1 - core)

    R = x_ref.shape[0]
    HR = R // 2
    D = x_ref.shape[1]
    FS = w1.shape[1]
    BLK = 2 * SIDE * R
    OWN = SIDE * R
    C = D // 2
    Q = C // 4

    cw1 = pltpu.make_async_copy(w1_hbm, w1, lsem.at[0])
    cw2 = pltpu.make_async_copy(w2_hbm, w2, lsem.at[1])
    cdy = pltpu.make_async_copy(dy_hbm, dy.at[pl.ds(0, R)], lsem.at[2])
    cdy.start()
    cw1.start()
    cw2.start()
    xhat, rstd = _ln(x_ref[...].astype(F32))
    xn[0:R, :] = (xhat * g_ref[...]).astype(BF16)

    bar = pltpu.get_barrier_semaphore()
    for d in (yp, ym, yf, xp, xm, xf, sib):
        pl.semaphore_signal(bar, inc=1, device_id=d, device_id_type=MESH)
    pl.semaphore_wait(bar, 7)

    def remote(src, dst, ss, rs, d):
        return pltpu.make_async_remote_copy(src_ref=src, dst_ref=dst, send_sem=ss, recv_sem=rs, device_id=d, device_id_type=MESH)

    pending = []

    def go(*cs):
        for c in cs:
            c.start()
            pending.append(c)

    def got(*cs):
        for c in cs:
            c.wait_recv()

    class Gather:
        def __init__(self, buf, first, second, xfirst, base):
            n = [base]

            def at(a, b, half=None):
                dd, ee = (b, a) if xfirst else (a, b)
                o = (IX[dd] * 2 * SIDE + IX[ee]) * R
                if half is None:
                    return buf.at[pl.ds(o, R)]
                return buf.at[pl.ds(o + half * HR, HR)]

            def mk(src, dst, d):
                i = n[0]
                n[0] += 1
                return remote(src, dst, ags.at[i], agr.at[i], d)

            (fp, fm), (sp, sm) = first, second
            self.d1 = (mk(at(0, 0), at(-1, 0), fp), mk(at(0, 0), at(1, 0), fm))
            self.d1h = (mk(at(-1, 0, 0), at(2, 0, 0), fp), mk(at(1, 0, 1), at(2, 0, 1), fm))
            self.d2 = {r: (mk(at(r, 0), at(r, -1), sp), mk(at(r, 0), at(r, 1), sm)) for r in REL}
            self.d2h = {r: (mk(at(r, -1, 0), at(r, 2, 0), sp), mk(at(r, 1, 1), at(r, 2, 1), sm)) for r in REL}
            self.sb = {r: mk(buf.at[pl.ds(IX[r] * BLK, OWN)], buf.at[pl.ds(IX[r] * BLK + OWN, OWN)], sib) for r in REL}

        def hop1(self):
            for c, n in zip(self.d1, self.d1h):
                got(c)
                go(n)

        def hop2(self, r):
            for c, n in zip(self.d2[r], self.d2h[r]):
                got(c)
                go(n)

    TF = FS // 2

    def keep(dd, f):
        if dd == 1:
            return [[acc.at[1, 2 * f + j, 1 + c] for j in range(2)] for c in range(2)]
        if dd == 2:
            return [[zbuf.at[c, 2 * f + j] for j in range(2)] for c in range(2)]
        return [[dwst.at[c, :, pl.ds(pl.multiple_of(f * TF + j * Q, Q), Q)] for j in range(2)] for c in range(2)]

    def hidden(dd, forward, backward):
        o = IX[dd] * BLK

        def step(f, _):
            fo = pl.multiple_of(f * TF, TF)
            if forward:
                a = _dot(xn[o:o + BLK, :], w1[:, pl.ds(fo, TF)], 1, 0)
                hv, gv = _gelu_and_grad(a)
                h[o:o + BLK, pl.ds(fo, TF)] = hv.astype(BF16)
                if not backward:
                    for c, row in enumerate(keep(dd, f)):
                        for j, ref in enumerate(row):
                            ref[...] = a[c * OWN:(c + 1) * OWN, j * Q:(j + 1) * Q].reshape(ref.shape)
            if backward:
                dh = _dot(dy[o:o + BLK, :], w2[pl.ds(fo, TF), :], 1, 1)
                if forward:
                    da[o:o + BLK, pl.ds(fo, TF)] = (gv * dh).astype(BF16)
                else:
                    for c, row in enumerate(keep(dd, f)):
                        for j, ref in enumerate(row):
                            gv = _gelu_and_grad(ref[...].reshape(OWN, Q))[1]
                            co = pl.multiple_of(fo + j * Q, Q)
                            da[o + c * OWN:o + (c + 1) * OWN, pl.ds(co, Q)] = (
                                gv * dh[c * OWN:(c + 1) * OWN, j * Q:(j + 1) * Q]).astype(BF16)
            return 0

        lax.fori_loop(0, FS // TF, step, 0)

    ROUND = ((0, 0), (1, 0), (1, 1), (0, 1))
    live = {}
    slots = [None, None]
    count = [0]

    def mblk(k, i):
        s, slot, o = k % 2, count[0] % 2, i * BLK
        back, half = ROUND[k]
        count[0] += 1
        if slots[slot] is not None:
            slots[slot].wait_send()

        def step(n, _):
            co = pl.multiple_of(half * C + n * (2 * Q), 2 * Q)
            if back:
                t = _dot(da[o:o + BLK, :], w1[pl.ds(co, 2 * Q), :], 1, 1)
            else:
                t = _dot(h[o:o + BLK, :], w2[:, pl.ds(co, 2 * Q)], 1, 0)
            for j in range(2):
                acc[s, 2 * n + j, i] = t[:OWN, j * Q:(j + 1) * Q].reshape(SIDE, R, Q)
                stage[slot, 2 * n + j] = t[OWN:, j * Q:(j + 1) * Q].reshape(SIDE, R, Q)
            return 0

        lax.fori_loop(0, 2, step, 0)
        if k > 0:
            pl.semaphore_wait(csib.at[i], 1)
        c = remote(stage.at[slot], sibr.at[i], sbs.at[slot], sbr.at[i], sib)
        c.start()
        slots[slot] = c
        live["sib", k, i] = c

    def add(k, i):
        live.pop(("sib", k, i)).wait_recv()
        for q in range(4):
            acc[k % 2, q, i] = acc[k % 2, q, i] + sibr[i, q]
        if k < 3:
            pl.semaphore_signal(csib.at[i], inc=1, device_id=sib, device_id_type=MESH)

    YR, XR = (yp, ym), (xp, xm)

    def ring_copies(get, buf, ss, rs, ring, parts=1):
        plus, minus = ring
        src = [(get(0, 2), plus), (get(1, 2), minus), (get(1, 1), plus), (get(0, -1), minus), (get(0, 1), plus), (get(1, -1), minus)]
        out = []
        for j, (v, d) in enumerate(src):
            if parts == 1 or j > 3:
                out.append([remote(v, buf.at[j], ss.at[j, 0], rs.at[j, 0], d)])
            else:
                n = SIDE // parts
                out.append([remote(v.at[pl.ds(c * n, n)], buf.at[j, pl.ds(c * n, n)], ss.at[j, c], rs.at[j, c], d) for c in range(parts)])
        return out

    def p1_get(k, ab):
        if ab == 0:
            return lambda p, r: acc.at[k % 2, p, IX[r]]
        return lambda p, r: acc.at[k % 2, 2 + p, :, IX[r]]

    def p2_get(k, ab):
        return lambda p, r: zbuf.at[k % 2, 2 * ab + p, IX[r]]

    def begin(k):
        if k >= 2:
            for i in range(4):
                pl.semaphore_wait(c1.at[i], 1)
        s = k % 2
        live["c1", k] = [ring_copies(p1_get(k, ab), r1.at[s, ab], p1s.at[s, ab], p1r.at[s, ab], (YR, XR)[ab], 1 + ab) for ab in range(2)]

    def send_a(k, js):
        for j in js:
            live["c1", k][0][j][0].start()

    def send_b(k, c):
        for j in range(4):
            live["c1", k][1][j][c].start()

    def e1(k):
        begin(k)
        for j in range(4):
            send_a(k, (j,))
            for c in live["c1", k][1][j]:
                c.start()

    def forward(get, buf, cs, ab):
        for j, p, r in ((0, 0, 1), (1, 1, -1)):
            got(*cs[ab][j])
            v = get(p, r)
            v[...] = v[...] + buf[ab, j]
            cs[ab][4 + j][0].start()

    def final(get, buf, cs, ab):
        for j in (2, 3, 4, 5):
            got(*cs[ab][j])
        return (get(0, 0)[...] + buf[ab, 3] + buf[ab, 4], get(1, 0)[...] + buf[ab, 2] + buf[ab, 5])

    def credit(c):
        for i, d in enumerate((ym, yp, xm, xp)):
            pl.semaphore_signal(c.at[i], inc=1, device_id=d, device_id_type=MESH)

    def drained(key):
        for v in live.pop(key):
            for cs in v:
                for c in cs:
                    c.wait_send()

    def e2(k):
        for ab in range(2):
            forward(p1_get(k, ab), r1.at[k % 2], live["c1", k], ab)

    def e3(k):
        s = k % 2
        if k >= 2:
            drained(("c2", k - 2))
            for i in range(4):
                pl.semaphore_wait(c2.at[i], 1)
        ds = [ring_copies(p2_get(k, ab), r2.at[s, ab], p2s.at[s, ab], p2r.at[s, ab], (XR, YR)[ab]) for ab in range(2)]
        live["c2", k] = ds
        for ab in range(2):
            a, b = final(p1_get(k, ab), r1.at[s], live["c1", k], ab)
            zbuf[s, 2 * ab] = a
            zbuf[s, 2 * ab + 1] = b
            for j in range(4):
                ds[ab][j][0].start()
        if k < 2:
            credit(c1)

    def e4(k):
        for ab in range(2):
            forward(p2_get(k, ab), r2.at[k % 2], live["c2", k], ab)

    def e5(k):
        back, half = ROUND[k]
        for ab in range(2):
            a, b = final(p2_get(k, ab), r2.at[k % 2], live["c2", k], ab)
            o = half * C + 2 * ab * Q
            ysum[back, :, o:o + Q] = a
            ysum[back, :, o + Q:o + 2 * Q] = b
        if k < 2:
            credit(c2)

    TM = dwst.shape[1]
    NT2 = FS // TM * (D // FS)
    NT1 = D // TM

    def dw2_copy(i):
        r = pl.multiple_of((i // 2) * TM, TM)
        c = pl.multiple_of((i % 2) * FS, FS)
        return pltpu.make_async_copy(dwst.at[i % 2], dw2_hbm.at[pl.ds(r, TM), pl.ds(c, FS)], lsem.at[3 + i % 2])

    def dw1_copy(i):
        r = pl.multiple_of(i * TM, TM)
        return pltpu.make_async_copy(dwst.at[i % 2], dw1_hbm.at[pl.ds(r, TM), :], lsem.at[3 + i % 2])

    def dw2_tile(i):
        r = pl.multiple_of((i // 2) * TM, TM)
        c = pl.multiple_of((i % 2) * FS, FS)
        return _dot(h[:, pl.ds(r, TM)], dy[:, pl.ds(c, FS)], 0, 0)

    def dw1_tile(i):
        r = pl.multiple_of(i * TM, TM)
        return _dot(xn[:, pl.ds(r, TM)], da[...], 0, 0)

    done = [0]

    def dw(n):
        i0 = done[0]
        done[0] += n
        copy, tile, lo, total = (dw2_copy, dw2_tile, i0, NT2) if i0 < NT2 else (dw1_copy, dw1_tile, i0 - NT2, NT1)
        hi = lo + n
        assert hi <= total

        def step(i, _):
            @pl.when(i >= 2)
            def _():
                copy(i - 2).wait()
            dwst[i % 2] = tile(i)
            copy(i).start()
            return 0

        lax.fori_loop(lo, hi, step, 0)
        if hi == total:
            copy(total - 2).wait()
            copy(total - 1).wait()

    gx = Gather(xn, (xp, xm), (yp, ym), True, 0)
    gy = Gather(dy, (yp, ym), (xp, xm), False, 24)

    cdy.wait()
    go(*gx.d1, *gy.d1)
    go(*gx.d2[0], *gy.d2[0])
    gx.hop1()
    gy.hop1()
    go(*gx.d2[-1], *gx.d2[1])
    gy.hop2(0)
    go(*gy.d2[1], *gy.d2[-1])
    got(*gx.d1h)
    go(*gx.d2[2], gx.sb[0])
    got(*gy.d2h[0])
    go(gy.sb[0])
    got(*gy.d1h)
    cw1.wait()
    cw2.wait()
    got(gx.sb[0], gy.sb[0])
    hidden(0, True, True)
    gy.hop2(1)
    go(*gy.d2[2])
    gx.hop2(0)
    gx.hop2(-1)
    mblk(0, 0)
    gx.hop2(1)
    add(0, 0)
    mblk(1, 0)
    gy.hop2(-1)
    add(1, 0)
    gx.hop2(2)
    go(gx.sb[1], gx.sb[-1])
    got(*gy.d2h[1])
    go(gy.sb[1])
    got(gx.sb[1])
    hidden(1, True, False)
    gy.hop2(2)
    mblk(0, 1)
    got(gx.sb[-1])
    hidden(-1, True, False)
    add(0, 1)
    begin(0)
    send_b(0, 0)
    mblk(0, 2)
    got(*gy.d2h[-1])
    go(gy.sb[-1])
    got(gy.sb[1])
    hidden(1, False, True)
    add(0, 2)
    send_a(0, (2, 3))
    for r in REL:
        got(*gx.d2h[r])
    go(gx.sb[2])
    got(*gy.d2h[2])
    go(gy.sb[2])
    got(gx.sb[2])
    hidden(2, True, False)
    mblk(0, 3)
    got(gy.sb[-1])
    hidden(-1, False, True)
    add(0, 3)
    send_a(0, (0, 1))
    send_b(0, 1)
    got(gy.sb[2])
    hidden(2, False, True)
    mblk(1, 1)
    e2(0)
    mblk(1, 2)
    add(1, 1)
    mblk(1, 3)
    add(1, 2)
    dw(2)
    add(1, 3)
    e1(1)
    e3(0)
    drained(("c1", 0))
    mblk(2, 0)
    mblk(2, 1)
    add(2, 0)
    mblk(2, 2)
    add(2, 1)
    e2(1)
    mblk(2, 3)
    add(2, 2)
    dw(2)
    add(2, 3)
    e1(2)
    e4(0)
    dw(2)
    e3(1)
    drained(("c1", 1))
    mblk(3, 0)
    mblk(3, 1)
    add(3, 0)
    mblk(3, 2)
    add(3, 1)
    mblk(3, 3)
    add(3, 2)
    dw(2)
    add(3, 3)
    e1(3)
    e2(2)
    e5(0)
    e4(1)
    dw(2)
    e3(2)
    e2(3)
    dw(2)
    e5(1)
    e4(2)
    e3(3)
    dw(2)

    xhat, rstd = _ln(x_ref[...].astype(F32))
    e5(2)
    dxn = ysum[1]
    gam[0] = jnp.sum(dxn * xhat, axis=0, keepdims=True)
    cs = [remote(gam.at[0], gin.at[0], gs.at[0], gr.at[0], sib)]
    cs += [remote(gam.at[1], gin.at[1 + j], gs.at[1 + j], gr.at[1 + j], d) for j, d in enumerate((xp, xm, xf))]
    cs += [remote(gam.at[2], gin.at[4 + j], gs.at[4 + j], gr.at[4 + j], d) for j, d in enumerate((yp, ym, yf))]
    go(cs[0])
    dxhat = dxn * g_ref[...]
    dx = rstd * (dxhat - jnp.mean(dxhat, axis=-1, keepdims=True) - xhat * jnp.mean(dxhat * xhat, axis=-1, keepdims=True))
    dx_out[...] = (dy[0:R, :].astype(F32) + dx).astype(BF16)
    got(cs[0])
    gam[1] = gam[0] + gin[0]
    go(*cs[1:4])
    e4(3)
    got(*cs[1:4])
    gam[2] = gam[1] + gin[1] + gin[2] + gin[3]
    go(*cs[4:7])
    dw(2)
    got(*cs[4:7])
    dg_out[...] = gam[2] + gin[4] + gin[5] + gin[6]
    e5(3)
    y_out[...] = (x_ref[...].astype(F32) + ysum[0]).astype(BF16)
    for c in pending + [v for v in slots]:
        c.wait_send()
    for key in (("c1", 2), ("c1", 3), ("c2", 2), ("c2", 3)):
        drained(key)


def _out_kernel(*refs):
    n = (len(refs) - 1) // 3
    src, dst, buf, sem = refs[:n], refs[n:2 * n], refs[2 * n:3 * n], refs[3 * n]
    reads, writes = [], []
    for s, d, b in zip(src, dst, buf):
        m = max(1, s.shape[0] * s.shape[1] * s.dtype.itemsize // 2 ** 20)
        r = s.shape[0] // m
        for i in range(m):
            j = len(reads)
            part = pl.ds(i * r, r)
            reads.append(pltpu.make_async_copy(s.at[part], b.at[part], sem.at[0, j]))
            writes.append(pltpu.make_async_copy(b.at[part], d.at[part], sem.at[1, j]))
    for c in reads:
        c.start()
    for c, w in zip(reads, writes):
        c.wait()
        w.start()
    for w in writes:
        w.wait()


def solution(mesh):
    rows = P(("data", "tp"), None)
    assert mesh.shape["tp"] == 2 * SIDE * SIDE

    def body(X, gamma, W1, W2, dY):
        R, D = X.shape
        FS = W1.shape[1]
        T = R * 2 * SIDE * SIDE
        C = D // 2
        Q = C // 4
        vm = pl.BlockSpec(memory_space=pltpu.VMEM)
        anyspace = pl.BlockSpec(memory_space=pl.ANY)
        dma = pltpu.SemaphoreType.DMA
        reg = pltpu.SemaphoreType.REGULAR
        raw = pl.pallas_call(
            _kernel,
            out_shape=(
                jax.ShapeDtypeStruct((R, D), BF16),
                jax.ShapeDtypeStruct((R, D), BF16),
                jax.ShapeDtypeStruct((1, D), F32),
                jax.ShapeDtypeStruct((D, FS), F32),
                jax.ShapeDtypeStruct((FS, D), F32),
            ),
            in_specs=[vm, vm, anyspace, anyspace, anyspace],
            out_specs=(vm, vm, vm, anyspace, anyspace),
            scratch_shapes=[
                pltpu.VMEM((T, D), BF16),
                pltpu.VMEM((T, D), BF16),
                pltpu.VMEM((T, FS), BF16),
                pltpu.VMEM((T, FS), BF16),
                pltpu.VMEM((D, FS), BF16),
                pltpu.VMEM((FS, D), BF16),
                pltpu.VMEM((2, 4, SIDE, SIDE, R, Q), F32),
                pltpu.VMEM((2, 4, SIDE, R, Q), F32),
                pltpu.VMEM((2, 4, SIDE, R, Q), F32),
                pltpu.VMEM((SIDE, 4, SIDE, R, Q), F32),
                pltpu.VMEM((2, 2, 6, SIDE, R, Q), F32),
                pltpu.VMEM((2, 2, 6, R, Q), F32),
                pltpu.VMEM((2, R, D), F32),
                pltpu.VMEM((3, 1, D), F32),
                pltpu.VMEM((7, 1, D), F32),
                pltpu.VMEM((2, 256, FS), F32),
                dma((48,)), dma((48,)),
                dma((2, 2, 6, 2)), dma((2, 2, 6, 2)),
                dma((2, 2, 6, 1)), dma((2, 2, 6, 1)),
                dma((2,)), dma((SIDE,)),
                dma((7,)), dma((7,)),
                dma((5,)),
                reg((4,)), reg((4,)), reg((SIDE,)),
            ],
            compiler_params=pltpu.CompilerParams(
                collective_id=0, has_side_effects=True, vmem_limit_bytes=67043328),
        )(X, gamma.reshape(1, D), W1, W2, dY)
        Y, dX, dg, dW1, dW2 = pl.pallas_call(
            _out_kernel,
            out_shape=tuple(jax.ShapeDtypeStruct(v.shape, v.dtype) for v in raw),
            in_specs=[anyspace] * 5,
            out_specs=(anyspace,) * 5,
            scratch_shapes=[pltpu.VMEM(v.shape, v.dtype) for v in raw] + [dma((2, 32))],
        )(*raw)
        return Y, dX, dW1, dW2, dg.reshape(D)

    return jax.shard_map(body, mesh=mesh,
                         in_specs=(rows, P(None), P(None, "tp"), P("tp", None), rows),
                         out_specs=(rows, rows, P("data", "tp"), rows, P("data")),
                         check_vma=False)
```

time: 218 us -> 179 us (0.82)
  Pallas kernels: 201 us -> 178 us
  local copies, waits for them, and re-layouts: 16.1 us -> 0 us
    pallas_call x1, Pallas kernels: 201 us -> 165 us  [body(): pl.pallas_call(_kernel, out_shape=(jax.ShapeDtypeStruct((R, D), BF16), ja...]
    unnamed x11 -> x0, local copies, waits for them, and re-layouts: 16.1 us -> none
    pallas_call x0 -> x1, Pallas kernels: none -> 12.4 us  [body(): pl.pallas_call(_out_kernel, out_shape=tuple((jax.ShapeDtypeStruct(v.shape...]
where the time goes in v2:
time: 179 us
  Pallas kernels  178 us (99%)
    pallas_call x1, Pallas kernels, body(): pl.pallas_call(_kernel, out_shape=(jax.ShapeDtypeStruct((R, D), BF16), ja...  165 us
    pallas_call x1, Pallas kernels, body(): pl.pallas_call(_out_kernel, out_shape=tuple((jax.ShapeDtypeStruct(v.shape...  12.4 us

profile of v2, /device:TPU:97, one launch (start us, length us, event | category | flops | bytes accessed | tf_op | source)
XLA Modules:
  0.0 178.6 jit_solution(17510874279773447028)
XLA Ops:
  0.6 165.4 %shard_map.92 = (bf16[64,2048]{1,0:T(8,128)(2,1)}, bf16[64,2048]{1,0:T(8,128)(2,1)}, f32[1,2048]{1,0:T(1,128)}, f32[2048,1024]{1,0:T(8,128)}, f32[1024,2048]{1,0:T(8,128)}) custom-call(bf16[64,2048]{1,0:T(8,128)(2,1)} %x_ref.1, f32[1,2048]{1,0:T(1,128)} %bitcast.2, bf16[2048,1024]{1,0:T(8,128)(2,1)} %w1_hbm.1, bf16[1024,2048]{1,0:T(8,128)(2,1)} %w2_hbm.1, ...), custom_call_target="tpu_custom_call" | custom-call | tf_op jit(solution)/shard_map/pallas_call | solution.py:525
  166.1 12.4 %shard_map.93 = (bf16[64,2048]{1,0:T(8,128)(2,1)}, bf16[64,2048]{1,0:T(8,128)(2,1)}, f32[1,2048]{1,0:T(1,128)}, f32[2048,1024]{1,0:T(8,128)}, f32[1024,2048]{1,0:T(8,128)}) custom-call(bf16[64,2048]{1,0:T(8,128)(2,1)} %get-tuple-element.15.refs_0_, bf16[64,2048]{1,0:T(8,128)(2,1)} %get-tuple-element.16.refs_1_, f32[1,2048]{1,0:T(1,128)} %get-tuple-element.17.refs_2_, ...), custom_call_target="tpu_custom_call" | custom-call | tf_op jit(solution)/shard_map/pallas_call | solution.py:564

commit v3 on v2

--- a/solution.py
+++ b/solution.py
@@ -92,16 +92,16 @@
         for c in cs:
             c.wait_recv()
 
-    class Gather:
-        def __init__(self, buf, first, second, xfirst, base):
+    class Half:
+        def __init__(self, buf, col, first, second, xfirst, base):
             n = [base]
 
             def at(a, b, half=None):
                 dd, ee = (b, a) if xfirst else (a, b)
                 o = (IX[dd] * 2 * SIDE + IX[ee]) * R
                 if half is None:
-                    return buf.at[pl.ds(o, R)]
-                return buf.at[pl.ds(o + half * HR, HR)]
+                    return buf.at[pl.ds(o, R), pl.ds(col, C)]
+                return buf.at[pl.ds(o + half * HR, HR), pl.ds(col, C)]
 
             def mk(src, dst, d):
                 i = n[0]
@@ -113,7 +113,6 @@
             self.d1h = (mk(at(-1, 0, 0), at(2, 0, 0), fp), mk(at(1, 0, 1), at(2, 0, 1), fm))
             self.d2 = {r: (mk(at(r, 0), at(r, -1), sp), mk(at(r, 0), at(r, 1), sm)) for r in REL}
             self.d2h = {r: (mk(at(r, -1, 0), at(r, 2, 0), sp), mk(at(r, 1, 1), at(r, 2, 1), sm)) for r in REL}
-            self.sb = {r: mk(buf.at[pl.ds(IX[r] * BLK, OWN)], buf.at[pl.ds(IX[r] * BLK + OWN, OWN)], sib) for r in REL}
 
         def hop1(self):
             for c, n in zip(self.d1, self.d1h):
@@ -125,39 +124,94 @@
                 got(c)
                 go(n)
 
+    class Gather:
+        def __init__(self, buf, base):
+            self.xy = Half(buf, 0, (xp, xm), (yp, ym), True, base)
+            self.yx = Half(buf, C, (yp, ym), (xp, xm), False, base + 20)
+            self.sb = {r: tuple(remote(buf.at[pl.ds(IX[r] * BLK + o, n)], buf.at[pl.ds(IX[r] * BLK + OWN + o, n)],
+                                       ags.at[base + 40 + 2 * IX[r] + j], agr.at[base + 40 + 2 * IX[r] + j], sib)
+                                for j, (o, n) in enumerate(((0, OWN - R), (OWN - R, R)))) for r in REL}
+
+        def s0(self):
+            go(*self.xy.d1, *self.yx.d1, *self.xy.d2[0], *self.yx.d2[0])
+
+        def s1(self):
+            self.xy.hop1()
+            self.yx.hop1()
+
+        def s1b(self):
+            for r in (1, -1):
+                go(*self.xy.d2[r], *self.yx.d2[r])
+
+        def s2(self):
+            self.xy.hop2(0)
+            self.yx.hop2(0)
+            go(self.sb[0][0])
+
+        def s3(self):
+            got(*self.xy.d1h, *self.yx.d1h)
+            go(*self.xy.d2[2], *self.yx.d2[2])
+
+        def s4(self):
+            got(*self.yx.d2h[0])
+            go(self.sb[0][1])
+
+        def s5(self):
+            for r in (1, -1):
+                self.xy.hop2(r)
+                self.yx.hop2(r)
+            go(self.sb[1][0], self.sb[-1][0])
+
+        def s6(self):
+            self.xy.hop2(2)
+            self.yx.hop2(2)
+
+        def s7(self):
+            for r in (1, -1):
+                got(*self.yx.d2h[r])
+                go(self.sb[r][1])
+
+        def s8(self):
+            got(*self.xy.d2h[0], *self.xy.d2h[1], *self.xy.d2h[-1])
+            go(self.sb[2][0])
+            got(*self.xy.d2h[2], *self.yx.d2h[2])
+            go(self.sb[2][1])
+
     TF = FS // 2
 
     def keep(dd, f):
-        if dd == 1:
-            return [[acc.at[1, 2 * f + j, 1 + c] for j in range(2)] for c in range(2)]
+        if dd in (0, 1):
+            return [[acc.at[1, 2 * f + j, (0, 3)[c] if dd == 0 else (1, 2)[c]] for j in range(2)] for c in range(2)]
         if dd == 2:
             return [[zbuf.at[c, 2 * f + j] for j in range(2)] for c in range(2)]
         return [[dwst.at[c, :, pl.ds(pl.multiple_of(f * TF + j * Q, Q), Q)] for j in range(2)] for c in range(2)]
 
-    def hidden(dd, forward, backward):
+    def forward_h(dd):
         o = IX[dd] * BLK
 
         def step(f, _):
             fo = pl.multiple_of(f * TF, TF)
-            if forward:
-                a = _dot(xn[o:o + BLK, :], w1[:, pl.ds(fo, TF)], 1, 0)
-                hv, gv = _gelu_and_grad(a)
-                h[o:o + BLK, pl.ds(fo, TF)] = hv.astype(BF16)
-                if not backward:
-                    for c, row in enumerate(keep(dd, f)):
-                        for j, ref in enumerate(row):
-                            ref[...] = a[c * OWN:(c + 1) * OWN, j * Q:(j + 1) * Q].reshape(ref.shape)
-            if backward:
-                dh = _dot(dy[o:o + BLK, :], w2[pl.ds(fo, TF), :], 1, 1)
-                if forward:
-                    da[o:o + BLK, pl.ds(fo, TF)] = (gv * dh).astype(BF16)
-                else:
-                    for c, row in enumerate(keep(dd, f)):
-                        for j, ref in enumerate(row):
-                            gv = _gelu_and_grad(ref[...].reshape(OWN, Q))[1]
-                            co = pl.multiple_of(fo + j * Q, Q)
-                            da[o + c * OWN:o + (c + 1) * OWN, pl.ds(co, Q)] = (
-                                gv * dh[c * OWN:(c + 1) * OWN, j * Q:(j + 1) * Q]).astype(BF16)
+            a = _dot(xn[o:o + BLK, :], w1[:, pl.ds(fo, TF)], 1, 0)
+            hv, gv = _gelu_and_grad(a)
+            h[o:o + BLK, pl.ds(fo, TF)] = hv.astype(BF16)
+            for c, row in enumerate(keep(dd, f)):
+                for j, ref in enumerate(row):
+                    ref[...] = gv[c * OWN:(c + 1) * OWN, j * Q:(j + 1) * Q].reshape(ref.shape)
+            return 0
+
+        lax.fori_loop(0, FS // TF, step, 0)
+
+    def backward_h(dd):
+        o = IX[dd] * BLK
+
+        def step(f, _):
+            fo = pl.multiple_of(f * TF, TF)
+            dh = _dot(dy[o:o + BLK, :], w2[pl.ds(fo, TF), :], 1, 1)
+            for c, row in enumerate(keep(dd, f)):
+                for j, ref in enumerate(row):
+                    co = pl.multiple_of(fo + j * Q, Q)
+                    da[o + c * OWN:o + (c + 1) * OWN, pl.ds(co, Q)] = (
+                        ref[...].reshape(OWN, Q) * dh[c * OWN:(c + 1) * OWN, j * Q:(j + 1) * Q]).astype(BF16)
             return 0
 
         lax.fori_loop(0, FS // TF, step, 0)
@@ -202,17 +256,10 @@
 
     YR, XR = (yp, ym), (xp, xm)
 
-    def ring_copies(get, buf, ss, rs, ring, parts=1):
+    def ring_copies(get, buf, ss, rs, ring):
         plus, minus = ring
         src = [(get(0, 2), plus), (get(1, 2), minus), (get(1, 1), plus), (get(0, -1), minus), (get(0, 1), plus), (get(1, -1), minus)]
-        out = []
-        for j, (v, d) in enumerate(src):
-            if parts == 1 or j > 3:
-                out.append([remote(v, buf.at[j], ss.at[j, 0], rs.at[j, 0], d)])
-            else:
-                n = SIDE // parts
-                out.append([remote(v.at[pl.ds(c * n, n)], buf.at[j, pl.ds(c * n, n)], ss.at[j, c], rs.at[j, c], d) for c in range(parts)])
-        return out
+        return [[remote(v, buf.at[j], ss.at[j], rs.at[j], d)] for j, (v, d) in enumerate(src)]
 
     def p1_get(k, ab):
         if ab == 0:
@@ -227,22 +274,17 @@
             for i in range(4):
                 pl.semaphore_wait(c1.at[i], 1)
         s = k % 2
-        live["c1", k] = [ring_copies(p1_get(k, ab), r1.at[s, ab], p1s.at[s, ab], p1r.at[s, ab], (YR, XR)[ab], 1 + ab) for ab in range(2)]
-
-    def send_a(k, js):
+        live["c1", k] = [ring_copies(p1_get(k, ab), r1.at[s, ab], p1s.at[s, ab], p1r.at[s, ab], (YR, XR)[ab]) for ab in range(2)]
+
+    def send_p1(k, js):
         for j in js:
-            live["c1", k][0][j][0].start()
-
-    def send_b(k, c):
-        for j in range(4):
-            live["c1", k][1][j][c].start()
+            for ab in range(2):
+                for c in live["c1", k][ab][j]:
+                    c.start()
 
     def e1(k):
         begin(k)
-        for j in range(4):
-            send_a(k, (j,))
-            for c in live["c1", k][1][j]:
-                c.start()
+        send_p1(k, range(4))
 
     def forward(get, buf, cs, ab):
         for j, p, r in ((0, 0, 1), (1, 1, -1)):
@@ -266,8 +308,8 @@
                 for c in cs:
                     c.wait_send()
 
-    def e2(k):
-        for ab in range(2):
+    def e2(k, abs_=(0, 1)):
+        for ab in abs_:
             forward(p1_get(k, ab), r1.at[k % 2], live["c1", k], ab)
 
     def e3(k):
@@ -345,77 +387,65 @@
             copy(total - 2).wait()
             copy(total - 1).wait()
 
-    gx = Gather(xn, (xp, xm), (yp, ym), True, 0)
-    gy = Gather(dy, (yp, ym), (xp, xm), False, 24)
-
+    gx = Gather(xn, 0)
+    gy = Gather(dy, 48)
+
+    gx.s0()
+    gx.s1()
+    gx.s2()
+    gx.s1b()
+    gx.s3()
+    gx.s4()
+    cw1.wait()
+    got(*gx.sb[0])
+    forward_h(0)
+    gx.s5()
+    cw2.wait()
+    mblk(0, 0)
+    gx.s6()
     cdy.wait()
-    go(*gx.d1, *gy.d1)
-    go(*gx.d2[0], *gy.d2[0])
-    gx.hop1()
-    gy.hop1()
-    go(*gx.d2[-1], *gx.d2[1])
-    gy.hop2(0)
-    go(*gy.d2[1], *gy.d2[-1])
-    got(*gx.d1h)
-    go(*gx.d2[2], gx.sb[0])
-    got(*gy.d2h[0])
-    go(gy.sb[0])
-    got(*gy.d1h)
-    cw1.wait()
-    cw2.wait()
-    got(gx.sb[0], gy.sb[0])
-    hidden(0, True, True)
-    gy.hop2(1)
-    go(*gy.d2[2])
-    gx.hop2(0)
-    gx.hop2(-1)
-    mblk(0, 0)
-    gx.hop2(1)
+    gy.s0()
+    gx.s7()
+    gx.s8()
     add(0, 0)
+    got(*gx.sb[1])
+    forward_h(1)
+    gy.s1()
+    gy.s2()
+    gy.s1b()
+    mblk(0, 1)
+    got(*gx.sb[-1])
+    forward_h(-1)
+    gy.s3()
+    mblk(0, 2)
+    add(0, 1)
+    got(*gx.sb[2])
+    forward_h(2)
+    add(0, 2)
+    gy.s4()
+    mblk(0, 3)
+    gy.s5()
+    got(*gy.sb[0])
+    backward_h(0)
+    add(0, 3)
+    gy.s6()
+    e1(0)
     mblk(1, 0)
-    gy.hop2(-1)
+    gy.s7()
+    gy.s8()
+    got(*gy.sb[1])
+    backward_h(1)
     add(1, 0)
-    gx.hop2(2)
-    go(gx.sb[1], gx.sb[-1])
-    got(*gy.d2h[1])
-    go(gy.sb[1])
-    got(gx.sb[1])
-    hidden(1, True, False)
-    gy.hop2(2)
-    mblk(0, 1)
-    got(gx.sb[-1])
-    hidden(-1, True, False)
-    add(0, 1)
-    begin(0)
-    send_b(0, 0)
-    mblk(0, 2)
-    got(*gy.d2h[-1])
-    go(gy.sb[-1])
-    got(gy.sb[1])
-    hidden(1, False, True)
-    add(0, 2)
-    send_a(0, (2, 3))
-    for r in REL:
-        got(*gx.d2h[r])
-    go(gx.sb[2])
-    got(*gy.d2h[2])
-    go(gy.sb[2])
-    got(gx.sb[2])
-    hidden(2, True, False)
-    mblk(0, 3)
-    got(gy.sb[-1])
-    hidden(-1, False, True)
-    add(0, 3)
-    send_a(0, (0, 1))
-    send_b(0, 1)
-    got(gy.sb[2])
-    hidden(2, False, True)
     mblk(1, 1)
+    got(*gy.sb[-1])
+    backward_h(-1)
+    add(1, 1)
     e2(0)
     mblk(1, 2)
-    add(1, 1)
+    got(*gy.sb[2])
+    backward_h(2)
+    add(1, 2)
     mblk(1, 3)
-    add(1, 2)
     dw(2)
     add(1, 3)
     e1(1)
@@ -445,17 +475,18 @@
     add(3, 2)
     dw(2)
     add(3, 3)
-    e1(3)
     e2(2)
+    e4(1)
+    begin(3)
+    send_p1(3, (0, 1))
     e5(0)
-    e4(1)
-    dw(2)
+    dw(4)
     e3(2)
-    e2(3)
+    send_p1(3, (2, 3))
     dw(2)
     e5(1)
     e4(2)
-    e3(3)
+    e2(3)
     dw(2)
 
     xhat, rstd = _ln(x_ref[...].astype(F32))
@@ -466,6 +497,7 @@
     cs += [remote(gam.at[1], gin.at[1 + j], gs.at[1 + j], gr.at[1 + j], d) for j, d in enumerate((xp, xm, xf))]
     cs += [remote(gam.at[2], gin.at[4 + j], gs.at[4 + j], gr.at[4 + j], d) for j, d in enumerate((yp, ym, yf))]
     go(cs[0])
+    e3(3)
     dxhat = dxn * g_ref[...]
     dx = rstd * (dxhat - jnp.mean(dxhat, axis=-1, keepdims=True) - xhat * jnp.mean(dxhat * xhat, axis=-1, keepdims=True))
     dx_out[...] = (dy[0:R, :].astype(F32) + dx).astype(BF16)
@@ -476,11 +508,10 @@
     got(*cs[1:4])
     gam[2] = gam[1] + gin[1] + gin[2] + gin[3]
     go(*cs[4:7])
-    dw(2)
+    e5(3)
+    y_out[...] = (x_ref[...].astype(F32) + ysum[0]).astype(BF16)
     got(*cs[4:7])
     dg_out[...] = gam[2] + gin[4] + gin[5] + gin[6]
-    e5(3)
-    y_out[...] = (x_ref[...].astype(F32) + ysum[0]).astype(BF16)
     for c in pending + [v for v in slots]:
         c.wait_send()
     for key in (("c1", 2), ("c1", 3), ("c2", 2), ("c2", 3)):
@@ -550,9 +581,9 @@
                 pltpu.VMEM((3, 1, D), F32),
                 pltpu.VMEM((7, 1, D), F32),
                 pltpu.VMEM((2, 256, FS), F32),
-                dma((48,)), dma((48,)),
-                dma((2, 2, 6, 2)), dma((2, 2, 6, 2)),
-                dma((2, 2, 6, 1)), dma((2, 2, 6, 1)),
+                dma((96,)), dma((96,)),
+                dma((2, 2, 6)), dma((2, 2, 6)),
+                dma((2, 2, 6)), dma((2, 2, 6)),
                 dma((2,)), dma((SIDE,)),
                 dma((7,)), dma((7,)),
                 dma((5,)),

time: 179 us -> 164 us (0.916)
  Pallas kernels: 178 us -> 163 us
    pallas_call x1, Pallas kernels: 165 us -> 150 us  [body(): pl.pallas_call(_kernel, out_shape=(jax.ShapeDtypeStruct((R, D), BF16), ja...]
where the time goes in v3:
time: 164 us
  Pallas kernels  163 us (99%)
    pallas_call x1, Pallas kernels, body(): pl.pallas_call(_kernel, out_shape=(jax.ShapeDtypeStruct((R, D), BF16), ja...  150 us
    pallas_call x1, Pallas kernels, body(): pl.pallas_call(_out_kernel, out_shape=tuple((jax.ShapeDtypeStruct(v.shape...  12.4 us

profile of v3, /device:TPU:97, one launch (start us, length us, event | category | flops | bytes accessed | tf_op | source)
XLA Modules:
  0.0 163.5 jit_solution(13292816552935494858)
XLA Ops:
  0.6 150.3 %shard_map.92 = (bf16[64,2048]{1,0:T(8,128)(2,1)}, bf16[64,2048]{1,0:T(8,128)(2,1)}, f32[1,2048]{1,0:T(1,128)}, f32[2048,1024]{1,0:T(8,128)}, f32[1024,2048]{1,0:T(8,128)}) custom-call(bf16[64,2048]{1,0:T(8,128)(2,1)} %x_ref.1, f32[1,2048]{1,0:T(1,128)} %bitcast.2, bf16[2048,1024]{1,0:T(8,128)(2,1)} %w1_hbm.1, bf16[1024,2048]{1,0:T(8,128)(2,1)} %w2_hbm.1, ...), custom_call_target="tpu_custom_call" | custom-call | tf_op jit(solution)/shard_map/pallas_call | solution.py:556
  151.0 12.4 %shard_map.93 = (bf16[64,2048]{1,0:T(8,128)(2,1)}, bf16[64,2048]{1,0:T(8,128)(2,1)}, f32[1,2048]{1,0:T(1,128)}, f32[2048,1024]{1,0:T(8,128)}, f32[1024,2048]{1,0:T(8,128)}) custom-call(bf16[64,2048]{1,0:T(8,128)(2,1)} %get-tuple-element.15.refs_0_, bf16[64,2048]{1,0:T(8,128)(2,1)} %get-tuple-element.16.refs_1_, f32[1,2048]{1,0:T(1,128)} %get-tuple-element.17.refs_2_, ...), custom_call_target="tpu_custom_call" | custom-call | tf_op jit(solution)/shard_map/pallas_call | solution.py:595

commit v4 on v3

--- a/solution.py
+++ b/solution.py
@@ -106,7 +106,7 @@
             def mk(src, dst, d):
                 i = n[0]
                 n[0] += 1
-                return remote(src, dst, ags.at[i], agr.at[i], d)
+                return remote(src, dst, ags.at[base // 48], agr.at[i], d)
 
             (fp, fm), (sp, sm) = first, second
             self.d1 = (mk(at(0, 0), at(-1, 0), fp), mk(at(0, 0), at(1, 0), fm))
@@ -129,7 +129,7 @@
             self.xy = Half(buf, 0, (xp, xm), (yp, ym), True, base)
             self.yx = Half(buf, C, (yp, ym), (xp, xm), False, base + 20)
             self.sb = {r: tuple(remote(buf.at[pl.ds(IX[r] * BLK + o, n)], buf.at[pl.ds(IX[r] * BLK + OWN + o, n)],
-                                       ags.at[base + 40 + 2 * IX[r] + j], agr.at[base + 40 + 2 * IX[r] + j], sib)
+                                       ags.at[base // 48], agr.at[base + 40 + 2 * IX[r] + j], sib)
                                 for j, (o, n) in enumerate(((0, OWN - R), (OWN - R, R)))) for r in REL}
 
         def s0(self):
@@ -256,10 +256,20 @@
 
     YR, XR = (yp, ym), (xp, xm)
 
-    def ring_copies(get, buf, ss, rs, ring):
+    def ring_copies(get, buf, ss, rs, ring, cut=0, early=False):
         plus, minus = ring
         src = [(get(0, 2), plus), (get(1, 2), minus), (get(1, 1), plus), (get(0, -1), minus), (get(0, 1), plus), (get(1, -1), minus)]
-        return [[remote(v, buf.at[j], ss.at[j], rs.at[j], d)] for j, (v, d) in enumerate(src)]
+        out = [[remote(v, buf.at[j], ss, rs.at[j], d)] for j, (v, d) in enumerate(src[:6 - 2 * cut])]
+        if early:
+            for j in range(4):
+                v, d = src[j]
+                out[j] = [remote(v.at[pl.ds(o, n)], buf.at[j, pl.ds(o, n)], ss, rs.at[j + 8 * c], d)
+                          for c, (o, n) in enumerate(((0, 3), (3, 1)))]
+        for j in range(6 - 2 * cut, 6):
+            v, d = src[j]
+            out.append([remote(v.at[pl.ds(o, 2)], buf.at[j, pl.ds(o, 2)], ss, rs.at[j + 2 * c], d)
+                        for c, o in enumerate((2, 0))])
+        return out
 
     def p1_get(k, ab):
         if ab == 0:
@@ -274,7 +284,7 @@
             for i in range(4):
                 pl.semaphore_wait(c1.at[i], 1)
         s = k % 2
-        live["c1", k] = [ring_copies(p1_get(k, ab), r1.at[s, ab], p1s.at[s, ab], p1r.at[s, ab], (YR, XR)[ab]) for ab in range(2)]
+        live["c1", k] = [ring_copies(p1_get(k, ab), r1.at[s, ab], p1s.at[s], p1r.at[s, ab], (YR, XR)[ab], k // 3, ab == 1 and k < 2) for ab in range(2)]
 
     def send_p1(k, js):
         for j in js:
@@ -286,12 +296,28 @@
         begin(k)
         send_p1(k, range(4))
 
+    def e1_early(k):
+        begin(k)
+        a, b = live["c1", k]
+        for j in range(4):
+            b[j][0].start()
+        for j in (2, 3):
+            a[j][0].start()
+
+    def e1_late(k):
+        a, b = live["c1", k]
+        for j in (0, 1):
+            a[j][0].start()
+        for j in range(4):
+            b[j][1].start()
+
     def forward(get, buf, cs, ab):
         for j, p, r in ((0, 0, 1), (1, 1, -1)):
             got(*cs[ab][j])
             v = get(p, r)
             v[...] = v[...] + buf[ab, j]
-            cs[ab][4 + j][0].start()
+            for c in cs[ab][4 + j]:
+                c.start()
 
     def final(get, buf, cs, ab):
         for j in (2, 3, 4, 5):
@@ -303,10 +329,10 @@
             pl.semaphore_signal(c.at[i], inc=1, device_id=d, device_id_type=MESH)
 
     def drained(key):
-        for v in live.pop(key):
-            for cs in v:
-                for c in cs:
-                    c.wait_send()
+        live.pop(key)
+        buf, ss = {"c1": (r1, p1s), "c2": (r2, p2s)}[key[0]]
+        s = key[1] % 2
+        pltpu.make_async_copy(buf.at[s], buf.at[s], ss.at[s]).wait()
 
     def e2(k, abs_=(0, 1)):
         for ab in abs_:
@@ -318,7 +344,7 @@
             drained(("c2", k - 2))
             for i in range(4):
                 pl.semaphore_wait(c2.at[i], 1)
-        ds = [ring_copies(p2_get(k, ab), r2.at[s, ab], p2s.at[s, ab], p2r.at[s, ab], (XR, YR)[ab]) for ab in range(2)]
+        ds = [ring_copies(p2_get(k, ab), r2.at[s, ab], p2s.at[s], p2r.at[s, ab], (XR, YR)[ab]) for ab in range(2)]
         live["c2", k] = ds
         for ab in range(2):
             a, b = final(p1_get(k, ab), r1.at[s], live["c1", k], ab)
@@ -328,6 +354,23 @@
                 ds[ab][j][0].start()
         if k < 2:
             credit(c1)
+
+    def e3_last(k, c):
+        s = k % 2
+        if c == 0:
+            drained(("c2", k - 2))
+            for i in range(4):
+                pl.semaphore_wait(c2.at[i], 1)
+            live["c2", k] = [ring_copies(p2_get(k, ab), r2.at[s, ab], p2s.at[s], p2r.at[s, ab], (XR, YR)[ab]) for ab in range(2)]
+        for ab in range(2):
+            cs, get, o = live["c1", k][ab], p1_get(k, ab), pl.ds(2 - 2 * c, 2)
+            if c == 0:
+                got(*cs[2], *cs[3])
+            for p, ja, jb in ((0, 3, 4), (1, 2, 5)):
+                got(cs[jb][c])
+                zbuf[s, 2 * ab + p, o] = get(p, 0)[o] + r1[s, ab, ja, o] + r1[s, ab, jb, o]
+            for j in ((0, 1, 3), (2,))[c]:
+                live["c2", k][ab][j][0].start()
 
     def e4(k):
         for ab in range(2):
@@ -419,24 +462,25 @@
     gy.s3()
     mblk(0, 2)
     add(0, 1)
+    gy.s4()
     got(*gx.sb[2])
     forward_h(2)
+    gy.s5()
     add(0, 2)
-    gy.s4()
+    e1_early(0)
     mblk(0, 3)
-    gy.s5()
+    gy.s6()
     got(*gy.sb[0])
     backward_h(0)
     add(0, 3)
-    gy.s6()
-    e1(0)
+    e1_late(0)
     mblk(1, 0)
     gy.s7()
-    gy.s8()
     got(*gy.sb[1])
     backward_h(1)
     add(1, 0)
     mblk(1, 1)
+    gy.s8()
     got(*gy.sb[-1])
     backward_h(-1)
     add(1, 1)
@@ -446,9 +490,10 @@
     backward_h(2)
     add(1, 2)
     mblk(1, 3)
+    e1_early(1)
     dw(2)
     add(1, 3)
-    e1(1)
+    e1_late(1)
     e3(0)
     drained(("c1", 0))
     mblk(2, 0)
@@ -456,9 +501,9 @@
     add(2, 0)
     mblk(2, 2)
     add(2, 1)
-    e2(1)
     mblk(2, 3)
     add(2, 2)
+    e2(1)
     dw(2)
     add(2, 3)
     e1(2)
@@ -488,6 +533,10 @@
     e4(2)
     e2(3)
     dw(2)
+    for i, buf in enumerate((xn, dy)):
+        all_sent = buf.at[pl.ds(0, 31 * R)]
+        pltpu.make_async_copy(all_sent, all_sent, ags.at[i]).wait()
+    pending.clear()
 
     xhat, rstd = _ln(x_ref[...].astype(F32))
     e5(2)
@@ -497,17 +546,18 @@
     cs += [remote(gam.at[1], gin.at[1 + j], gs.at[1 + j], gr.at[1 + j], d) for j, d in enumerate((xp, xm, xf))]
     cs += [remote(gam.at[2], gin.at[4 + j], gs.at[4 + j], gr.at[4 + j], d) for j, d in enumerate((yp, ym, yf))]
     go(cs[0])
-    e3(3)
     dxhat = dxn * g_ref[...]
     dx = rstd * (dxhat - jnp.mean(dxhat, axis=-1, keepdims=True) - xhat * jnp.mean(dxhat * xhat, axis=-1, keepdims=True))
     dx_out[...] = (dy[0:R, :].astype(F32) + dx).astype(BF16)
     got(cs[0])
     gam[1] = gam[0] + gin[0]
     go(*cs[1:4])
-    e4(3)
+    e3_last(3, 0)
+    e3_last(3, 1)
     got(*cs[1:4])
     gam[2] = gam[1] + gin[1] + gin[2] + gin[3]
     go(*cs[4:7])
+    e4(3)
     e5(3)
     y_out[...] = (x_ref[...].astype(F32) + ysum[0]).astype(BF16)
     got(*cs[4:7])
@@ -581,9 +631,9 @@
                 pltpu.VMEM((3, 1, D), F32),
                 pltpu.VMEM((7, 1, D), F32),
                 pltpu.VMEM((2, 256, FS), F32),
-                dma((96,)), dma((96,)),
-                dma((2, 2, 6)), dma((2, 2, 6)),
-                dma((2, 2, 6)), dma((2, 2, 6)),
+                dma((2,)), dma((96,)),
+                dma((2,)), dma((2, 2, 12)),
+                dma((2,)), dma((2, 2, 6)),
                 dma((2,)), dma((SIDE,)),
                 dma((7,)), dma((7,)),
                 dma((5,)),

time: 164 us -> 160 us (0.976)
  Pallas kernels: 163 us -> 159 us
    pallas_call x1, Pallas kernels: 150 us -> 147 us  [body(): pl.pallas_call(_kernel, out_shape=(jax.ShapeDtypeStruct((R, D), BF16), ja...]
where the time goes in v4:
time: 160 us
  Pallas kernels  159 us (99%)
    pallas_call x1, Pallas kernels, body(): pl.pallas_call(_kernel, out_shape=(jax.ShapeDtypeStruct((R, D), BF16), ja...  147 us
    pallas_call x1, Pallas kernels, body(): pl.pallas_call(_out_kernel, out_shape=tuple((jax.ShapeDtypeStruct(v.shape...  12.4 us

profile of v4, /device:TPU:97, one launch (start us, length us, event | category | flops | bytes accessed | tf_op | source)
XLA Modules:
  0.0 159.8 jit_solution(14572814718281166460)
XLA Ops:
  0.6 146.6 %shard_map.92 = (bf16[64,2048]{1,0:T(8,128)(2,1)}, bf16[64,2048]{1,0:T(8,128)(2,1)}, f32[1,2048]{1,0:T(1,128)}, f32[2048,1024]{1,0:T(8,128)}, f32[1024,2048]{1,0:T(8,128)}) custom-call(bf16[64,2048]{1,0:T(8,128)(2,1)} %x_ref.1, f32[1,2048]{1,0:T(1,128)} %bitcast.2, bf16[2048,1024]{1,0:T(8,128)(2,1)} %w1_hbm.1, bf16[1024,2048]{1,0:T(8,128)(2,1)} %w2_hbm.1, ...), custom_call_target="tpu_custom_call" | custom-call | tf_op jit(solution)/shard_map/pallas_call | solution.py:606
  147.3 12.4 %shard_map.93 = (bf16[64,2048]{1,0:T(8,128)(2,1)}, bf16[64,2048]{1,0:T(8,128)(2,1)}, f32[1,2048]{1,0:T(1,128)}, f32[2048,1024]{1,0:T(8,128)}, f32[1024,2048]{1,0:T(8,128)}) custom-call(bf16[64,2048]{1,0:T(8,128)(2,1)} %get-tuple-element.15.refs_0_, bf16[64,2048]{1,0:T(8,128)(2,1)} %get-tuple-element.16.refs_1_, f32[1,2048]{1,0:T(1,128)} %get-tuple-element.17.refs_2_, ...), custom_call_target="tpu_custom_call" | custom-call | tf_op jit(solution)/shard_map/pallas_call | solution.py:645

commit v5 on v4

--- a/solution.py
+++ b/solution.py
@@ -40,8 +40,8 @@
 
 
 def _kernel(x_ref, g_ref, w1_hbm, w2_hbm, dy_hbm,
-            y_out, dx_out, dg_out, dw1_hbm, dw2_hbm,
-            xn, dy, h, da, w1, w2, acc, zbuf, stage, sibr, r1, r2, ysum, gam, gin, dwst,
+            y_out, dx_out, dg_out, acc, sibr, dw2_hbm,
+            xn, dy, h, da, w1, w2, zbuf, stage, r1, r2, ysum, gam, gin, dwst,
             ags, agr, p1s, p1r, p2s, p2r, sbs, sbr, gs, gr, lsem, c1, c2, csib):
     me = lax.axis_index("tp")
     core = me % 2
@@ -395,10 +395,6 @@
         c = pl.multiple_of((i % 2) * FS, FS)
         return pltpu.make_async_copy(dwst.at[i % 2], dw2_hbm.at[pl.ds(r, TM), pl.ds(c, FS)], lsem.at[3 + i % 2])
 
-    def dw1_copy(i):
-        r = pl.multiple_of(i * TM, TM)
-        return pltpu.make_async_copy(dwst.at[i % 2], dw1_hbm.at[pl.ds(r, TM), :], lsem.at[3 + i % 2])
-
     def dw2_tile(i):
         r = pl.multiple_of((i // 2) * TM, TM)
         c = pl.multiple_of((i % 2) * FS, FS)
@@ -413,22 +409,32 @@
     def dw(n):
         i0 = done[0]
         done[0] += n
-        copy, tile, lo, total = (dw2_copy, dw2_tile, i0, NT2) if i0 < NT2 else (dw1_copy, dw1_tile, i0 - NT2, NT1)
+        lo, total = (i0, NT2) if i0 < NT2 else (i0 - NT2, NT1)
         hi = lo + n
         assert hi <= total
 
-        def step(i, _):
+        def step2(i, _):
             @pl.when(i >= 2)
             def _():
-                copy(i - 2).wait()
-            dwst[i % 2] = tile(i)
-            copy(i).start()
+                dw2_copy(i - 2).wait()
+            dwst[i % 2] = dw2_tile(i)
+            dw2_copy(i).start()
             return 0
 
-        lax.fori_loop(lo, hi, step, 0)
-        if hi == total:
-            copy(total - 2).wait()
-            copy(total - 1).wait()
+        def step1(i, _):
+            t = dw1_tile(i)
+            for q in range(4):
+                v = t[:, q * Q:(q + 1) * Q].reshape(SIDE, R, Q)
+                if hi <= SIDE:
+                    sibr[i, q] = v
+                else:
+                    acc[0, q, i - SIDE] = v
+            return 0
+
+        lax.fori_loop(lo, hi, step2 if i0 < NT2 else step1, 0)
+        if i0 < NT2 and hi == total:
+            dw2_copy(total - 2).wait()
+            dw2_copy(total - 1).wait()
 
     gx = Gather(xn, 0)
     gy = Gather(dy, 48)
@@ -528,6 +534,7 @@
     dw(4)
     e3(2)
     send_p1(3, (2, 3))
+    drained(("c1", 2))
     dw(2)
     e5(1)
     e4(2)
@@ -564,15 +571,14 @@
     dg_out[...] = gam[2] + gin[4] + gin[5] + gin[6]
     for c in pending + [v for v in slots]:
         c.wait_send()
-    for key in (("c1", 2), ("c1", 3), ("c2", 2), ("c2", 3)):
+    for key in (("c1", 3), ("c2", 2), ("c2", 3)):
         drained(key)
 
 
-def _out_kernel(*refs):
-    n = (len(refs) - 1) // 3
-    src, dst, buf, sem = refs[:n], refs[n:2 * n], refs[2 * n:3 * n], refs[3 * n]
+def _out_kernel(y, dx, dg, acc, sibr, dw2, y_out, dx_out, dg_out, dw1_out, dw2_out, by, bdx, bdg, bdw2, sem, one):
+    _, P4, _, S4, R, Q = acc.shape
     reads, writes = [], []
-    for s, d, b in zip(src, dst, buf):
+    for s, d, b in ((dw2, dw2_out, bdw2), (y, y_out, by), (dx, dx_out, bdx), (dg, dg_out, bdg)):
         m = max(1, s.shape[0] * s.shape[1] * s.dtype.itemsize // 2 ** 20)
         r = s.shape[0] // m
         for i in range(m):
@@ -582,11 +588,16 @@
             writes.append(pltpu.make_async_copy(b.at[part], d.at[part], sem.at[1, j]))
     for c in reads:
         c.start()
+    for t in range(2 * S4):
+        for q in range(P4):
+            src = sibr.at[t, q] if t < S4 else acc.at[0, q, t - S4]
+            pltpu.make_async_copy(src, dw1_out.at[pl.ds(t * S4, S4), :, pl.ds(q * Q, Q)], one.at[0]).start()
     for c, w in zip(reads, writes):
         c.wait()
         w.start()
     for w in writes:
         w.wait()
+    pltpu.make_async_copy(dw1_out, dw1_out, one.at[0]).wait()
 
 
 def solution(mesh):
@@ -609,11 +620,12 @@
                 jax.ShapeDtypeStruct((R, D), BF16),
                 jax.ShapeDtypeStruct((R, D), BF16),
                 jax.ShapeDtypeStruct((1, D), F32),
-                jax.ShapeDtypeStruct((D, FS), F32),
+                pltpu.VMEM((2, 4, SIDE, SIDE, R, Q), F32),
+                pltpu.VMEM((SIDE, 4, SIDE, R, Q), F32),
                 jax.ShapeDtypeStruct((FS, D), F32),
             ),
             in_specs=[vm, vm, anyspace, anyspace, anyspace],
-            out_specs=(vm, vm, vm, anyspace, anyspace),
+            out_specs=(vm, vm, vm, vm, vm, anyspace),
             scratch_shapes=[
                 pltpu.VMEM((T, D), BF16),
                 pltpu.VMEM((T, D), BF16),
@@ -621,10 +633,8 @@
                 pltpu.VMEM((T, FS), BF16),
                 pltpu.VMEM((D, FS), BF16),
                 pltpu.VMEM((FS, D), BF16),
-                pltpu.VMEM((2, 4, SIDE, SIDE, R, Q), F32),
                 pltpu.VMEM((2, 4, SIDE, R, Q), F32),
                 pltpu.VMEM((2, 4, SIDE, R, Q), F32),
-                pltpu.VMEM((SIDE, 4, SIDE, R, Q), F32),
                 pltpu.VMEM((2, 2, 6, SIDE, R, Q), F32),
                 pltpu.VMEM((2, 2, 6, R, Q), F32),
                 pltpu.VMEM((2, R, D), F32),
@@ -640,16 +650,28 @@
                 reg((4,)), reg((4,)), reg((SIDE,)),
             ],
             compiler_params=pltpu.CompilerParams(
-                collective_id=0, has_side_effects=True, vmem_limit_bytes=67043328),
+                collective_id=0, has_side_effects=True, vmem_limit_bytes=67043328 - 12 * 2 ** 20 - 2 ** 17),
         )(X, gamma.reshape(1, D), W1, W2, dY)
+        Y, dX, dg, acc, sibr, dW2 = raw
+        acc = pltpu.with_memory_space_constraint(acc, pltpu.VMEM)
+        sibr = pltpu.with_memory_space_constraint(sibr, pltpu.VMEM)
+        Y, dX, dg, dW2 = (pltpu.with_memory_space_constraint(v, pltpu.HBM) for v in (Y, dX, dg, dW2))
         Y, dX, dg, dW1, dW2 = pl.pallas_call(
             _out_kernel,
-            out_shape=tuple(jax.ShapeDtypeStruct(v.shape, v.dtype) for v in raw),
-            in_specs=[anyspace] * 5,
+            out_shape=(
+                jax.ShapeDtypeStruct((R, D), BF16),
+                jax.ShapeDtypeStruct((R, D), BF16),
+                jax.ShapeDtypeStruct((1, D), F32),
+                jax.ShapeDtypeStruct((D // R, R, FS), F32),
+                jax.ShapeDtypeStruct((FS, D), F32),
+            ),
+            in_specs=[anyspace, anyspace, anyspace, vm, vm, anyspace],
             out_specs=(anyspace,) * 5,
-            scratch_shapes=[pltpu.VMEM(v.shape, v.dtype) for v in raw] + [dma((2, 32))],
-        )(*raw)
-        return Y, dX, dW1, dW2, dg.reshape(D)
+            scratch_shapes=[pltpu.VMEM((R, D), BF16), pltpu.VMEM((R, D), BF16), pltpu.VMEM((1, D), F32),
+                            pltpu.VMEM((FS, D), F32), dma((2, 16)), dma((1,))],
+            compiler_params=pltpu.CompilerParams(vmem_limit_bytes=67043328 - 12 * 2 ** 20 - 2 ** 17),
+        )(Y, dX, dg, acc, sibr, dW2)
+        return Y, dX, dW1.reshape(D, FS), dW2, dg.reshape(D)
 
     return jax.shard_map(body, mesh=mesh,
                          in_specs=(rows, P(None), P(None, "tp"), P("tp", None), rows),

time: 160 us -> 157 us (0.981)
  Pallas kernels: 159 us -> 156 us
    pallas_call x1, Pallas kernels: 12.4 us -> 9.61 us  [body(): pl.pallas_call(_out_kernel, out_shape=(jax.ShapeDtypeStruct((R, D), BF16)...]
where the time goes in v5:
time: 157 us
  Pallas kernels  156 us (99%)
    pallas_call x1, Pallas kernels, body(): pl.pallas_call(_kernel, out_shape=(jax.ShapeDtypeStruct((R, D), BF16), ja...  147 us
    pallas_call x1, Pallas kernels, body(): pl.pallas_call(_out_kernel, out_shape=(jax.ShapeDtypeStruct((R, D), BF16)...  9.61 us

profile of v5, /device:TPU:97, one launch (start us, length us, event | category | flops | bytes accessed | tf_op | source)
XLA Modules:
  0.0 157.1 jit_solution(2128565694238883362)
XLA Ops:
  0.6 146.7 %shard_map.92 = (bf16[64,2048]{1,0:T(8,128)(2,1)}, bf16[64,2048]{1,0:T(8,128)(2,1)}, f32[1,2048]{1,0:T(1,128)}, f32[2,4,4,4,64,256]{5,4,3,2,1,0:T(8,128)S(1)}, f...) custom-call(bf16[64,2048]{1,0:T(8,128)(2,1)} %x_ref.1, f32[1,2048]{1,0:T(1,128)} %bitcast.3, ...), custom_call_target="tpu_custom_call" | custom-call | tf_op jit(solution)/shard_map/pallas_call | solution.py:617
  147.3 9.6 %shard_map.93 = (bf16[64,2048]{1,0:T(8,128)(2,1)}, bf16[64,2048]{1,0:T(8,128)(2,1)}, f32[1,2048]{1,0:T(1,128)}, f32[32,64,1024]{2,1,0:T(8,128)}, f32[1024,2048]{1,0:T(8,128)}) custom-call(bf16[64,2048]{1,0:T(8,128)(2,1)} %get-tuple-element.16.y, bf16[64,2048]{1,0:T(8,128)(2,1)} %get-tuple-element.17.dx, f32[1,2048]{1,0:T(1,128)} %get-tuple-element.18.dg, ...), custom_call_target="tpu_custom_call" | custom-call | tf_op jit(solution)/shard_map/pallas_call | solution.py:659

commit v6 on v5

--- a/solution.py
+++ b/solution.py
@@ -40,8 +40,8 @@
 
 
 def _kernel(x_ref, g_ref, w1_hbm, w2_hbm, dy_hbm,
-            y_out, dx_out, dg_out, acc, sibr, dw2_hbm,
-            xn, dy, h, da, w1, w2, zbuf, stage, r1, r2, ysum, gam, gin, dwst,
+            y_out, dx_out, dg_out, acc, sibr, dwst, dw2_hbm,
+            xn, dy, h, da, w1, w2, zbuf, stage, r1, r2, ysum, gam, gin,
             ags, agr, p1s, p1r, p2s, p2r, sbs, sbr, gs, gr, lsem, c1, c2, csib):
     me = lax.axis_index("tp")
     core = me % 2
@@ -418,7 +418,8 @@
             def _():
                 dw2_copy(i - 2).wait()
             dwst[i % 2] = dw2_tile(i)
-            dw2_copy(i).start()
+            if lo < NT2 - 2:
+                dw2_copy(i).start()
             return 0
 
         def step1(i, _):
@@ -432,9 +433,6 @@
             return 0
 
         lax.fori_loop(lo, hi, step2 if i0 < NT2 else step1, 0)
-        if i0 < NT2 and hi == total:
-            dw2_copy(total - 2).wait()
-            dw2_copy(total - 1).wait()
 
     gx = Gather(xn, 0)
     gy = Gather(dy, 48)
@@ -575,10 +573,11 @@
         drained(key)
 
 
-def _out_kernel(y, dx, dg, acc, sibr, dw2, y_out, dx_out, dg_out, dw1_out, dw2_out, by, bdx, bdg, bdw2, sem, one):
+def _out_kernel(y, dx, dg, acc, sibr, dwst, dw2, y_out, dx_out, dg_out, dw1_out, dw2_out, by, bdx, bdg, bdw2, sem, one):
     _, P4, _, S4, R, Q = acc.shape
+    keep = dw2.shape[0] - dwst.shape[1]
     reads, writes = [], []
-    for s, d, b in ((dw2, dw2_out, bdw2), (y, y_out, by), (dx, dx_out, bdx), (dg, dg_out, bdg)):
+    for s, d, b in ((dw2.at[pl.ds(0, keep)], dw2_out, bdw2), (y, y_out, by), (dx, dx_out, bdx), (dg, dg_out, bdg)):
         m = max(1, s.shape[0] * s.shape[1] * s.dtype.itemsize // 2 ** 20)
         r = s.shape[0] // m
         for i in range(m):
@@ -588,6 +587,10 @@
             writes.append(pltpu.make_async_copy(b.at[part], d.at[part], sem.at[1, j]))
     for c in reads:
         c.start()
+    W = dwst.shape[2]
+    tail = [pltpu.make_async_copy(dwst.at[c], dw2_out.at[pl.ds(keep, dwst.shape[1]), pl.ds(c * W, W)], one.at[1 + c]) for c in range(2)]
+    for c in tail:
+        c.start()
     for t in range(2 * S4):
         for q in range(P4):
             src = sibr.at[t, q] if t < S4 else acc.at[0, q, t - S4]
@@ -595,7 +598,7 @@
     for c, w in zip(reads, writes):
         c.wait()
         w.start()
-    for w in writes:
+    for w in writes + tail:
         w.wait()
     pltpu.make_async_copy(dw1_out, dw1_out, one.at[0]).wait()
 
@@ -622,10 +625,11 @@
                 jax.ShapeDtypeStruct((1, D), F32),
                 pltpu.VMEM((2, 4, SIDE, SIDE, R, Q), F32),
                 pltpu.VMEM((SIDE, 4, SIDE, R, Q), F32),
+                pltpu.VMEM((2, 256, FS), F32),
                 jax.ShapeDtypeStruct((FS, D), F32),
             ),
             in_specs=[vm, vm, anyspace, anyspace, anyspace],
-            out_specs=(vm, vm, vm, vm, vm, anyspace),
+            out_specs=(vm, vm, vm, vm, vm, vm, anyspace),
             scratch_shapes=[
                 pltpu.VMEM((T, D), BF16),
                 pltpu.VMEM((T, D), BF16),
@@ -640,7 +644,6 @@
                 pltpu.VMEM((2, R, D), F32),
                 pltpu.VMEM((3, 1, D), F32),
                 pltpu.VMEM((7, 1, D), F32),
-                pltpu.VMEM((2, 256, FS), F32),
                 dma((2,)), dma((96,)),
                 dma((2,)), dma((2, 2, 12)),
                 dma((2,)), dma((2, 2, 6)),
@@ -650,9 +653,10 @@
                 reg((4,)), reg((4,)), reg((SIDE,)),
             ],
             compiler_params=pltpu.CompilerParams(
-                collective_id=0, has_side_effects=True, vmem_limit_bytes=67043328 - 12 * 2 ** 20 - 2 ** 17),
+                collective_id=0, has_side_effects=True, vmem_limit_bytes=67043328 - 14 * 2 ** 20 - 2 ** 17),
         )(X, gamma.reshape(1, D), W1, W2, dY)
-        Y, dX, dg, acc, sibr, dW2 = raw
+        Y, dX, dg, acc, sibr, dwst, dW2 = raw
+        dwst = pltpu.with_memory_space_constraint(dwst, pltpu.VMEM)
         acc = pltpu.with_memory_space_constraint(acc, pltpu.VMEM)
         sibr = pltpu.with_memory_space_constraint(sibr, pltpu.VMEM)
         Y, dX, dg, dW2 = (pltpu.with_memory_space_constraint(v, pltpu.HBM) for v in (Y, dX, dg, dW2))
@@ -665,12 +669,12 @@
                 jax.ShapeDtypeStruct((D // R, R, FS), F32),
                 jax.ShapeDtypeStruct((FS, D), F32),
             ),
-            in_specs=[anyspace, anyspace, anyspace, vm, vm, anyspace],
+            in_specs=[anyspace, anyspace, anyspace, vm, vm, vm, anyspace],
             out_specs=(anyspace,) * 5,
             scratch_shapes=[pltpu.VMEM((R, D), BF16), pltpu.VMEM((R, D), BF16), pltpu.VMEM((1, D), F32),
-                            pltpu.VMEM((FS, D), F32), dma((2, 16)), dma((1,))],
-            compiler_params=pltpu.CompilerParams(vmem_limit_bytes=67043328 - 12 * 2 ** 20 - 2 ** 17),
-        )(Y, dX, dg, acc, sibr, dW2)
+                            pltpu.VMEM((FS, D), F32), dma((2, 16)), dma((3,))],
+            compiler_params=pltpu.CompilerParams(vmem_limit_bytes=67043328 - 14 * 2 ** 20 - 2 ** 17),
+        )(Y, dX, dg, acc, sibr, dwst, dW2)
         return Y, dX, dW1.reshape(D, FS), dW2, dg.reshape(D)
 
     return jax.shard_map(body, mesh=mesh,

time: 157 us -> 156 us (level)
  no operation moved by 1% of the time
where the time goes in v6:
time: 156 us
  Pallas kernels  155 us (99%)
    pallas_call x1, Pallas kernels, body(): pl.pallas_call(_kernel, out_shape=(jax.ShapeDtypeStruct((R, D), BF16), ja...  146 us
    pallas_call x1, Pallas kernels, body(): pl.pallas_call(_out_kernel, out_shape=(jax.ShapeDtypeStruct((R, D), BF16)...  8.77 us

profile of v6, /device:TPU:97, one launch (start us, length us, event | category | flops | bytes accessed | tf_op | source)
XLA Modules:
  0.0 156.0 jit_solution(6467432938978121868)
XLA Ops:
  0.6 146.4 %shard_map.92 = (bf16[64,2048]{1,0:T(8,128)(2,1)}, bf16[64,2048]{1,0:T(8,128)(2,1)}, f32[1,2048]{1,0:T(1,128)}, f32[2,4,4,4,64,256]{5,4,3,2,1,0:T(8,128)S(1)}, f...) custom-call(bf16[64,2048]{1,0:T(8,128)(2,1)} %x_ref.1, f32[1,2048]{1,0:T(1,128)} %bitcast.3, ...), custom_call_target="tpu_custom_call" | custom-call | tf_op jit(solution)/shard_map/pallas_call | solution.py:620
  147.1 8.8 %shard_map.93 = (bf16[64,2048]{1,0:T(8,128)(2,1)}, bf16[64,2048]{1,0:T(8,128)(2,1)}, f32[1,2048]{1,0:T(1,128)}, f32[32,64,1024]{2,1,0:T(8,128)}, f32[1024,2048]{1,0:T(8,128)}) custom-call(bf16[64,2048]{1,0:T(8,128)(2,1)} %get-tuple-element.17.y, bf16[64,2048]{1,0:T(8,128)(2,1)} %get-tuple-element.18.dx, f32[1,2048]{1,0:T(1,128)} %get-tuple-element.19.dg, ...), custom_call_target="tpu_custom_call" | custom-call | tf_op jit(solution)/shard_map/pallas_call | solution.py:663
